TPU v7x, 8 devices: a whole 2x2x1 slice. The times are simulated.
8 devices in a mesh: py: 2 (over z, y), px: 4 (over x, core).
Axes of the slice: x: 2, y: 2, z: 1, core: 2. Of those that a mesh axis runs over, the one named last changes fastest.
Arguments:
- shift: float32 [256, 512, 24], P('px', 'py')
- rhs_field: float32 [256, 512, 24], P('px', 'py')
- x_init: float32 [256, 512, 24], P('px', 'py')
- cond_x: float32 [256, 512, 24], P('px', 'py')
- cond_y: float32 [256, 512, 24], P('px', 'py')
- cond_z: float32 [256, 512, 24], P('px', 'py')
Outputs:
- output 1: float32 [256, 512, 24], P('px', 'py')
- output 2: float32 [21], replicated
All inputs are finite; a program needn't handle non-finite values.
Results may differ from a plain program's by a relative error of at most 0.001.
Values sent between devices are 32-bit elements.
A program may use at most 1 GiB of HBM per device.

v0:
```python
import jax
import jax.numpy as jnp
from jax import lax
from jax.sharding import PartitionSpec as P

ITERS = 20
SUM_AXES = ("px", "py")


def solution(mesh):
    count_x = mesh.shape["px"]
    count_y = mesh.shape["py"]
    fwd_x = [(src, src + 1) for src in range(count_x - 1)]
    back_x = [(src + 1, src) for src in range(count_x - 1)]
    fwd_y = [(src, src + 1) for src in range(count_y - 1)]
    back_y = [(src + 1, src) for src in range(count_y - 1)]
    field_spec = P("px", "py", None)

    def local_solve(shift, rhs_field, x_init, cond_x, cond_y, cond_z):
        blk_x, blk_y, blk_z = shift.shape
        pos_x = lax.axis_index("px")
        pos_y = lax.axis_index("py")
        plane_x = lax.broadcasted_iota(jnp.int32, (blk_x, 1, 1), 0)
        plane_y = lax.broadcasted_iota(jnp.int32, (1, blk_y, 1), 1)
        plane_z = lax.broadcasted_iota(jnp.int32, (1, 1, blk_z), 2)
        plus_x = jnp.where((pos_x == count_x - 1) & (plane_x == blk_x - 1), 0.0, cond_x)
        plus_y = jnp.where((pos_y == count_y - 1) & (plane_y == blk_y - 1), 0.0, cond_y)
        plus_z = jnp.where(plane_z == blk_z - 1, 0.0, cond_z)
        minus_x = jnp.concatenate([lax.ppermute(plus_x[-1:], "px", fwd_x), plus_x[:-1]], axis=0)
        minus_y = jnp.concatenate([lax.ppermute(plus_y[:, -1:], "py", fwd_y), plus_y[:, :-1]], axis=1)
        minus_z = jnp.concatenate([jnp.zeros_like(plus_z[:, :, :1]), plus_z[:, :, :-1]], axis=2)
        diag_coef = shift + plus_x + minus_x + plus_y + minus_y + plus_z + minus_z

        def apply_op(vec):
            low_x = lax.ppermute(vec[-1:], "px", fwd_x)
            high_x = lax.ppermute(vec[:1], "px", back_x)
            low_y = lax.ppermute(vec[:, -1:], "py", fwd_y)
            high_y = lax.ppermute(vec[:, :1], "py", back_y)
            zero_z = jnp.zeros_like(vec[:, :, :1])
            up_x = jnp.concatenate([vec[1:], high_x], axis=0)
            down_x = jnp.concatenate([low_x, vec[:-1]], axis=0)
            up_y = jnp.concatenate([vec[:, 1:], high_y], axis=1)
            down_y = jnp.concatenate([low_y, vec[:, :-1]], axis=1)
            up_z = jnp.concatenate([vec[:, :, 1:], zero_z], axis=2)
            down_z = jnp.concatenate([zero_z, vec[:, :, :-1]], axis=2)
            return (diag_coef * vec - plus_x * up_x - minus_x * down_x
                    - plus_y * up_y - minus_y * down_y - plus_z * up_z - minus_z * down_z)

        def global_dot(left, right):
            return lax.psum(jnp.sum(left * right), SUM_AXES)

        total_cells = blk_x * blk_y * blk_z * count_x * count_y
        x_cur = x_init
        r_cur = rhs_field - apply_op(x_init)
        p_cur = r_cur
        rho_cur = global_dot(r_cur, r_cur)
        rho_list = [rho_cur]
        for step_idx in range(ITERS):
            q_vec = apply_op(p_cur)
            step_alpha = rho_cur / global_dot(p_cur, q_vec)
            x_cur = x_cur + step_alpha * p_cur
            r_cur = r_cur - step_alpha * q_vec
            rho_new = global_dot(r_cur, r_cur)
            p_cur = r_cur + (rho_new / rho_cur) * p_cur
            rho_cur = rho_new
            rho_list.append(rho_cur)
        history = jnp.sqrt(jnp.stack(rho_list) / total_cells)
        return x_cur, history

    return jax.shard_map(local_solve, mesh=mesh, in_specs=(field_spec,) * 6,
                         out_specs=(field_spec, P()), check_vma=False)
```

profile of v0, /device:TPU:0, one launch (start us, length us, event | category | flops | bytes accessed | tf_op | source)
XLA Modules:
  0.0 1856.3 jit_solution(6161919858746424903)
XLA Ops:
  80.4 24.2 %all-reduce.43 = (f32[]{:T(128)}, f32[]{:T(128)}) all-reduce(f32[]{:T(128)} %get-tuple-element.5, f32[]{:T(128)} %get-tuple-element.4), channel_id=1, replica_groups=mesh['py'=2,'px'=4] {'px','py'}, use_global_device_ids=true, to_apply=%region_1.2 | all-reduce | flops 2 | bytes 16 | tf_op jit(solution)/shard_map/psum | solution.py:50
  108.8 23.3 %psum.289 = f32[]{:T(128)} all-reduce(f32[]{:T(128)} %multiply_reduce_fusion.38), channel_id=1, replica_groups=mesh['py'=2,'px'=4] {'px','py'}, use_global_device_ids=true, to_apply=%region_5.6 | all-reduce | flops 1 | bytes 8 | tf_op jit(solution)/shard_map/psum | solution.py:50
  170.6 24.0 %psum.290 = f32[]{:T(128)} all-reduce(f32[]{:T(128)} %get-tuple-element.80), channel_id=1, replica_groups=mesh['py'=2,'px'=4] {'px','py'}, use_global_device_ids=true, to_apply=%region_7.8 | all-reduce | flops 1 | bytes 8 | tf_op jit(solution)/shard_map/psum | solution.py:50
  200.5 23.2 %psum.291 = f32[]{:T(128)} all-reduce(f32[]{:T(128)} %get-tuple-element.78), channel_id=1, replica_groups=mesh['py'=2,'px'=4] {'px','py'}, use_global_device_ids=true, to_apply=%region_9.10 | all-reduce | flops 1 | bytes 8 | tf_op jit(solution)/shard_map/psum | solution.py:50
  289.2 24.4 %psum.293 = f32[]{:T(128)} all-reduce(f32[]{:T(128)} %get-tuple-element.74), channel_id=1, replica_groups=mesh['py'=2,'px'=4] {'px','py'}, use_global_device_ids=true, to_apply=%region_13.14 | all-reduce | flops 1 | bytes 8 | tf_op jit(solution)/shard_map/psum | solution.py:50
  378.9 23.4 %psum.295 = f32[]{:T(128)} all-reduce(f32[]{:T(128)} %get-tuple-element.70), channel_id=1, replica_groups=mesh['py'=2,'px'=4] {'px','py'}, use_global_device_ids=true, to_apply=%region_17.18 | all-reduce | flops 1 | bytes 8 | tf_op jit(solution)/shard_map/psum | solution.py:50
  467.5 24.3 %psum.297 = f32[]{:T(128)} all-reduce(f32[]{:T(128)} %get-tuple-element.66), channel_id=1, replica_groups=mesh['py'=2,'px'=4] {'px','py'}, use_global_device_ids=true, to_apply=%region_21.22 | all-reduce | flops 1 | bytes 8 | tf_op jit(solution)/shard_map/psum | solution.py:50
  557.2 23.5 %psum.299 = f32[]{:T(128)} all-reduce(f32[]{:T(128)} %get-tuple-element.62), channel_id=1, replica_groups=mesh['py'=2,'px'=4] {'px','py'}, use_global_device_ids=true, to_apply=%region_25.26 | all-reduce | flops 1 | bytes 8 | tf_op jit(solution)/shard_map/psum | solution.py:50
  646.1 24.3 %psum.301 = f32[]{:T(128)} all-reduce(f32[]{:T(128)} %get-tuple-element.58), channel_id=1, replica_groups=mesh['py'=2,'px'=4] {'px','py'}, use_global_device_ids=true, to_apply=%region_29.30 | all-reduce | flops 1 | bytes 8 | tf_op jit(solution)/shard_map/psum | solution.py:50
  735.7 23.5 %psum.303 = f32[]{:T(128)} all-reduce(f32[]{:T(128)} %get-tuple-element.54), channel_id=1, replica_groups=mesh['py'=2,'px'=4] {'px','py'}, use_global_device_ids=true, to_apply=%region_33.34 | all-reduce | flops 1 | bytes 8 | tf_op jit(solution)/shard_map/psum | solution.py:50
  824.8 24.2 %psum.305 = f32[]{:T(128)} all-reduce(f32[]{:T(128)} %get-tuple-element.50), channel_id=1, replica_groups=mesh['py'=2,'px'=4] {'px','py'}, use_global_device_ids=true, to_apply=%region_37.38 | all-reduce | flops 1 | bytes 8 | tf_op jit(solution)/shard_map/psum | solution.py:50
  914.6 23.5 %psum.307 = f32[]{:T(128)} all-reduce(f32[]{:T(128)} %get-tuple-element.46), channel_id=1, replica_groups=mesh['py'=2,'px'=4] {'px','py'}, use_global_device_ids=true, to_apply=%region_41.42 | all-reduce | flops 1 | bytes 8 | tf_op jit(solution)/shard_map/psum | solution.py:50
  1003.7 24.2 %psum.309 = f32[]{:T(128)} all-reduce(f32[]{:T(128)} %get-tuple-element.42), channel_id=1, replica_groups=mesh['py'=2,'px'=4] {'px','py'}, use_global_device_ids=true, to_apply=%region_45.46 | all-reduce | flops 1 | bytes 8 | tf_op jit(solution)/shard_map/psum | solution.py:50
  1093.7 23.5 %psum.311 = f32[]{:T(128)} all-reduce(f32[]{:T(128)} %get-tuple-element.38), channel_id=1, replica_groups=mesh['py'=2,'px'=4] {'px','py'}, use_global_device_ids=true, to_apply=%region_49.50 | all-reduce | flops 1 | bytes 8 | tf_op jit(solution)/shard_map/psum | solution.py:50
  1182.7 24.3 %psum.313 = f32[]{:T(128)} all-reduce(f32[]{:T(128)} %get-tuple-element.34), channel_id=1, replica_groups=mesh['py'=2,'px'=4] {'px','py'}, use_global_device_ids=true, to_apply=%region_53.54 | all-reduce | flops 1 | bytes 8 | tf_op jit(solution)/shard_map/psum | solution.py:50
  1272.1 23.5 %psum.315 = f32[]{:T(128)} all-reduce(f32[]{:T(128)} %get-tuple-element.30), channel_id=1, replica_groups=mesh['py'=2,'px'=4] {'px','py'}, use_global_device_ids=true, to_apply=%region_57.58 | all-reduce | flops 1 | bytes 8 | tf_op jit(solution)/shard_map/psum | solution.py:50
  1361.1 24.2 %psum.317 = f32[]{:T(128)} all-reduce(f32[]{:T(128)} %get-tuple-element.26), channel_id=1, replica_groups=mesh['py'=2,'px'=4] {'px','py'}, use_global_device_ids=true, to_apply=%region_61.62 | all-reduce | flops 1 | bytes 8 | tf_op jit(solution)/shard_map/psum | solution.py:50
  1423.2 22.5 %psum.318 = f32[]{:T(128)} all-reduce(f32[]{:T(128)} %get-tuple-element.24), channel_id=1, replica_groups=mesh['py'=2,'px'=4] {'px','py'}, use_global_device_ids=true, to_apply=%region_63.64 | all-reduce | flops 1 | bytes 8 | tf_op jit(solution)/shard_map/psum | solution.py:50
  1450.8 23.4 %psum.319 = f32[]{:T(128)} all-reduce(f32[]{:T(128)} %get-tuple-element.22), channel_id=1, replica_groups=mesh['py'=2,'px'=4] {'px','py'}, use_global_device_ids=true, to_apply=%region_65.66 | all-reduce | flops 1 | bytes 8 | tf_op jit(solution)/shard_map/psum | solution.py:50
  1539.7 24.2 %psum.321 = f32[]{:T(128)} all-reduce(f32[]{:T(128)} %get-tuple-element.18), channel_id=1, replica_groups=mesh['py'=2,'px'=4] {'px','py'}, use_global_device_ids=true, to_apply=%region_69.70 | all-reduce | flops 1 | bytes 8 | tf_op jit(solution)/shard_map/psum | solution.py:50
  1629.2 23.5 %psum.323 = f32[]{:T(128)} all-reduce(f32[]{:T(128)} %get-tuple-element.14), channel_id=1, replica_groups=mesh['py'=2,'px'=4] {'px','py'}, use_global_device_ids=true, to_apply=%region_73.74 | all-reduce | flops 1 | bytes 8 | tf_op jit(solution)/shard_map/psum | solution.py:50
  1718.2 24.2 %psum.325 = f32[]{:T(128)} all-reduce(f32[]{:T(128)} %get-tuple-element.10), channel_id=1, replica_groups=mesh['py'=2,'px'=4] {'px','py'}, use_global_device_ids=true, to_apply=%region_77.78 | all-reduce | flops 1 | bytes 8 | tf_op jit(solution)/shard_map/psum | solution.py:50
  1780.9 22.4 %psum.326 = f32[]{:T(128)} all-reduce(f32[]{:T(128)} %get-tuple-element.8), channel_id=1, replica_groups=mesh['py'=2,'px'=4] {'px','py'}, use_global_device_ids=true, to_apply=%region_79.80 | all-reduce | flops 1 | bytes 8 | tf_op jit(solution)/shard_map/psum | solution.py:50
  1818.4 23.6 %psum.327 = f32[1]{0:T(128)} all-reduce(f32[1]{0:T(128)} %bitcast.20), channel_id=1, replica_groups=mesh['py'=2,'px'=4] {'px','py'}, use_global_device_ids=true, to_apply=%region_81.82 | all-reduce | flops 1 | bytes 8 | tf_op jit(solution)/shard_map/psum | solution.py:50
  (544 shorter events, 1234.0 us)
Async XLA Ops:
  1.4 37.1 %collective-permute-start.3 = (f32[1,256,24]{1,2,0:T(8,128)S(1)}, f32[1,256,24]{1,2,0:T(8,128)S(1)}, u32[]{:S(2)}, u32[]{:S(2)}) collective-permute-start(f32[1,256,24]{1,2,0:T(8,128)S(1)} %get-tuple-element.291), channel_id=1, source_target_pairs={{0,1},{1,2},{2,3},{4,5},{5,6},{6,7}} | collective-permute-start | bytes 73736 | tf_op jit(solution)/shard_map/ppermute | solution.py:35
  4.2 34.3 %collective-permute-start.2 = (f32[1,256,24]{1,2,0:T(8,128)S(1)}, f32[1,256,24]{1,2,0:T(8,128)S(1)}, u32[]{:S(2)}, u32[]{:S(2)}) collective-permute-start(f32[1,256,24]{1,2,0:T(8,128)S(1)} %get-tuple-element.292), channel_id=1, source_target_pairs={{1,0},{2,1},{3,2},{5,4},{6,5},{7,6}} | collective-permute-start | bytes 73736 | tf_op jit(solution)/shard_map/ppermute | solution.py:36
  7.2 31.2 %collective-permute-start = (f32[1,256,24]{1,2,0:T(8,128)S(1)}, f32[1,256,24]{1,2,0:T(8,128)S(1)}, u32[]{:S(2)}, u32[]{:S(2)}) collective-permute-start(f32[1,256,24]{1,2,0:T(8,128)S(1)} %slice.860), channel_id=1, source_target_pairs={{0,1},{1,2},{2,3},{4,5},{5,6},{6,7}} | collective-permute-start | bytes 73736 | tf_op jit(solution)/shard_map/ppermute | solution.py:29
  12.9 23.0 %collective-permute-start.4 = (f32[64,1,24]{0,2,1:T(8,128)S(1)}, f32[64,1,24]{0,2,1:T(8,128)S(1)}, u32[]{:S(2)}, u32[]{:S(2)}) collective-permute-start(f32[64,1,24]{0,2,1:T(8,128)S(1)} %copy.112), channel_id=1, source_target_pairs={{4,0},{5,1},{6,2},{7,3}} | collective-permute-start | bytes 18440 | tf_op jit(solution)/shard_map/ppermute | solution.py:38
  141.4 19.7 %collective-permute-start.10 = (f32[1,256,24]{1,2,0:T(8,128)S(1)}, f32[1,256,24]{1,2,0:T(8,128)S(1)}, u32[]{:S(2)}, u32[]{:S(2)}) collective-permute-start(f32[1,256,24]{1,2,0:T(8,128)S(1)} %get-tuple-element.267), channel_id=1, source_target_pairs={{1,0},{2,1},{3,2},{5,4},{6,5},{7,6}} | collective-permute-start | bytes 73736 | tf_op jit(solution)/shard_map/ppermute | solution.py:36
  232.3 19.8 %collective-permute-start.14 = (f32[1,256,24]{1,2,0:T(8,128)S(1)}, f32[1,256,24]{1,2,0:T(8,128)S(1)}, u32[]{:S(2)}, u32[]{:S(2)}) collective-permute-start(f32[1,256,24]{1,2,0:T(8,128)S(1)} %get-tuple-element.257), channel_id=1, source_target_pairs={{1,0},{2,1},{3,2},{5,4},{6,5},{7,6}} | collective-permute-start | bytes 73736 | tf_op jit(solution)/shard_map/ppermute | solution.py:36
  322.1 19.8 %collective-permute-start.18 = (f32[1,256,24]{1,2,0:T(8,128)S(1)}, f32[1,256,24]{1,2,0:T(8,128)S(1)}, u32[]{:S(2)}, u32[]{:S(2)}) collective-permute-start(f32[1,256,24]{1,2,0:T(8,128)S(1)} %get-tuple-element.247), channel_id=1, source_target_pairs={{1,0},{2,1},{3,2},{5,4},{6,5},{7,6}} | collective-permute-start | bytes 73736 | tf_op jit(solution)/shard_map/ppermute | solution.py:36
  410.8 19.8 %collective-permute-start.22 = (f32[1,256,24]{1,2,0:T(8,128)S(1)}, f32[1,256,24]{1,2,0:T(8,128)S(1)}, u32[]{:S(2)}, u32[]{:S(2)}) collective-permute-start(f32[1,256,24]{1,2,0:T(8,128)S(1)} %get-tuple-element.237), channel_id=1, source_target_pairs={{1,0},{2,1},{3,2},{5,4},{6,5},{7,6}} | collective-permute-start | bytes 73736 | tf_op jit(solution)/shard_map/ppermute | solution.py:36
  500.3 19.8 %collective-permute-start.26 = (f32[1,256,24]{1,2,0:T(8,128)S(1)}, f32[1,256,24]{1,2,0:T(8,128)S(1)}, u32[]{:S(2)}, u32[]{:S(2)}) collective-permute-start(f32[1,256,24]{1,2,0:T(8,128)S(1)} %get-tuple-element.227), channel_id=1, source_target_pairs={{1,0},{2,1},{3,2},{5,4},{6,5},{7,6}} | collective-permute-start | bytes 73736 | tf_op jit(solution)/shard_map/ppermute | solution.py:36
  589.3 19.8 %collective-permute-start.30 = (f32[1,256,24]{1,2,0:T(8,128)S(1)}, f32[1,256,24]{1,2,0:T(8,128)S(1)}, u32[]{:S(2)}, u32[]{:S(2)}) collective-permute-start(f32[1,256,24]{1,2,0:T(8,128)S(1)} %get-tuple-element.217), channel_id=1, source_target_pairs={{1,0},{2,1},{3,2},{5,4},{6,5},{7,6}} | collective-permute-start | bytes 73736 | tf_op jit(solution)/shard_map/ppermute | solution.py:36
  679.0 19.7 %collective-permute-start.34 = (f32[1,256,24]{1,2,0:T(8,128)S(1)}, f32[1,256,24]{1,2,0:T(8,128)S(1)}, u32[]{:S(2)}, u32[]{:S(2)}) collective-permute-start(f32[1,256,24]{1,2,0:T(8,128)S(1)} %get-tuple-element.207), channel_id=1, source_target_pairs={{1,0},{2,1},{3,2},{5,4},{6,5},{7,6}} | collective-permute-start | bytes 73736 | tf_op jit(solution)/shard_map/ppermute | solution.py:36
  767.9 19.9 %collective-permute-start.38 = (f32[1,256,24]{1,2,0:T(8,128)S(1)}, f32[1,256,24]{1,2,0:T(8,128)S(1)}, u32[]{:S(2)}, u32[]{:S(2)}) collective-permute-start(f32[1,256,24]{1,2,0:T(8,128)S(1)} %get-tuple-element.197), channel_id=1, source_target_pairs={{1,0},{2,1},{3,2},{5,4},{6,5},{7,6}} | collective-permute-start | bytes 73736 | tf_op jit(solution)/shard_map/ppermute | solution.py:36
  769.3 18.5 collective-permute-start.39
  857.7 19.8 %collective-permute-start.42 = (f32[1,256,24]{1,2,0:T(8,128)S(1)}, f32[1,256,24]{1,2,0:T(8,128)S(1)}, u32[]{:S(2)}, u32[]{:S(2)}) collective-permute-start(f32[1,256,24]{1,2,0:T(8,128)S(1)} %get-tuple-element.187), channel_id=1, source_target_pairs={{1,0},{2,1},{3,2},{5,4},{6,5},{7,6}} | collective-permute-start | bytes 73736 | tf_op jit(solution)/shard_map/ppermute | solution.py:36
  946.9 19.8 %collective-permute-start.46 = (f32[1,256,24]{1,2,0:T(8,128)S(1)}, f32[1,256,24]{1,2,0:T(8,128)S(1)}, u32[]{:S(2)}, u32[]{:S(2)}) collective-permute-start(f32[1,256,24]{1,2,0:T(8,128)S(1)} %get-tuple-element.177), channel_id=1, source_target_pairs={{1,0},{2,1},{3,2},{5,4},{6,5},{7,6}} | collective-permute-start | bytes 73736 | tf_op jit(solution)/shard_map/ppermute | solution.py:36
  1036.7 19.8 %collective-permute-start.50 = (f32[1,256,24]{1,2,0:T(8,128)S(1)}, f32[1,256,24]{1,2,0:T(8,128)S(1)}, u32[]{:S(2)}, u32[]{:S(2)}) collective-permute-start(f32[1,256,24]{1,2,0:T(8,128)S(1)} %get-tuple-element.167), channel_id=1, source_target_pairs={{1,0},{2,1},{3,2},{5,4},{6,5},{7,6}} | collective-permute-start | bytes 73736 | tf_op jit(solution)/shard_map/ppermute | solution.py:36
  1125.9 19.7 %collective-permute-start.54 = (f32[1,256,24]{1,2,0:T(8,128)S(1)}, f32[1,256,24]{1,2,0:T(8,128)S(1)}, u32[]{:S(2)}, u32[]{:S(2)}) collective-permute-start(f32[1,256,24]{1,2,0:T(8,128)S(1)} %get-tuple-element.157), channel_id=1, source_target_pairs={{1,0},{2,1},{3,2},{5,4},{6,5},{7,6}} | collective-permute-start | bytes 73736 | tf_op jit(solution)/shard_map/ppermute | solution.py:36
  1215.4 19.8 %collective-permute-start.58 = (f32[1,256,24]{1,2,0:T(8,128)S(1)}, f32[1,256,24]{1,2,0:T(8,128)S(1)}, u32[]{:S(2)}, u32[]{:S(2)}) collective-permute-start(f32[1,256,24]{1,2,0:T(8,128)S(1)} %get-tuple-element.147), channel_id=1, source_target_pairs={{1,0},{2,1},{3,2},{5,4},{6,5},{7,6}} | collective-permute-start | bytes 73736 | tf_op jit(solution)/shard_map/ppermute | solution.py:36
  1304.1 19.8 %collective-permute-start.62 = (f32[1,256,24]{1,2,0:T(8,128)S(1)}, f32[1,256,24]{1,2,0:T(8,128)S(1)}, u32[]{:S(2)}, u32[]{:S(2)}) collective-permute-start(f32[1,256,24]{1,2,0:T(8,128)S(1)} %get-tuple-element.137), channel_id=1, source_target_pairs={{1,0},{2,1},{3,2},{5,4},{6,5},{7,6}} | collective-permute-start | bytes 73736 | tf_op jit(solution)/shard_map/ppermute | solution.py:36
  1393.9 19.7 %collective-permute-start.66 = (f32[1,256,24]{1,2,0:T(8,128)S(1)}, f32[1,256,24]{1,2,0:T(8,128)S(1)}, u32[]{:S(2)}, u32[]{:S(2)}) collective-permute-start(f32[1,256,24]{1,2,0:T(8,128)S(1)} %get-tuple-element.127), channel_id=1, source_target_pairs={{1,0},{2,1},{3,2},{5,4},{6,5},{7,6}} | collective-permute-start | bytes 73736 | tf_op jit(solution)/shard_map/ppermute | solution.py:36
  1482.8 19.8 %collective-permute-start.70 = (f32[1,256,24]{1,2,0:T(8,128)S(1)}, f32[1,256,24]{1,2,0:T(8,128)S(1)}, u32[]{:S(2)}, u32[]{:S(2)}) collective-permute-start(f32[1,256,24]{1,2,0:T(8,128)S(1)} %get-tuple-element.117), channel_id=1, source_target_pairs={{1,0},{2,1},{3,2},{5,4},{6,5},{7,6}} | collective-permute-start | bytes 73736 | tf_op jit(solution)/shard_map/ppermute | solution.py:36
  1572.4 19.7 %collective-permute-start.74 = (f32[1,256,24]{1,2,0:T(8,128)S(1)}, f32[1,256,24]{1,2,0:T(8,128)S(1)}, u32[]{:S(2)}, u32[]{:S(2)}) collective-permute-start(f32[1,256,24]{1,2,0:T(8,128)S(1)} %get-tuple-element.107), channel_id=1, source_target_pairs={{1,0},{2,1},{3,2},{5,4},{6,5},{7,6}} | collective-permute-start | bytes 73736 | tf_op jit(solution)/shard_map/ppermute | solution.py:36
  1661.2 19.8 %collective-permute-start.78 = (f32[1,256,24]{1,2,0:T(8,128)S(1)}, f32[1,256,24]{1,2,0:T(8,128)S(1)}, u32[]{:S(2)}, u32[]{:S(2)}) collective-permute-start(f32[1,256,24]{1,2,0:T(8,128)S(1)} %get-tuple-element.97), channel_id=1, source_target_pairs={{1,0},{2,1},{3,2},{5,4},{6,5},{7,6}} | collective-permute-start | bytes 73736 | tf_op jit(solution)/shard_map/ppermute | solution.py:36
  1751.0 19.8 %collective-permute-start.82 = (f32[1,256,24]{1,2,0:T(8,128)S(1)}, f32[1,256,24]{1,2,0:T(8,128)S(1)}, u32[]{:S(2)}, u32[]{:S(2)}) collective-permute-start(f32[1,256,24]{1,2,0:T(8,128)S(1)} %get-tuple-element.87), channel_id=1, source_target_pairs={{1,0},{2,1},{3,2},{5,4},{6,5},{7,6}} | collective-permute-start | bytes 73736 | tf_op jit(solution)/shard_map/ppermute | solution.py:36
  (109 other events, 1279.5 us)
where the time goes:
time: 1870 us; the launch traced here: 1860 us
  blocking collectives  927 us (50%)
  other arithmetic  323 us (17%)
  local copies, waits for them, and re-layouts  292 us (16%)
  starting transfers between devices  219 us (12%)
  between operations  53.2 us (3%)
  waiting for transfers between devices  42.3 us (2%)
    psum x40, blocking collectives, global_dot(): return lax.psum(jnp.sum(left * right), SUM_AXES)  927 us
    reduce_sum x40, other arithmetic, global_dot(): return lax.psum(jnp.sum(left * right), SUM_AXES)  266 us
    ppermute x21, starting transfers between devices, apply_op(): low_y = lax.ppermute(vec[:, -1:], 'py', fwd_y)  89.7 us
    ppermute x21, starting transfers between devices, apply_op(): low_x = lax.ppermute(vec[-1:], 'px', fwd_x)  64.1 us
    slice x40, local copies, waits for them, and re-layouts, apply_op(): high_y = lax.ppermute(vec[:, :1], 'py', back_y)  60.4 us
    slice x20, local copies, waits for them, and re-layouts, apply_op(): up_y = jnp.concatenate([vec[:, 1:], high_y], axis=1)  43.5 us
    ppermute x21, waiting for transfers between devices, apply_op(): high_y = lax.ppermute(vec[:, :1], 'py', back_y)  42.1 us
    slice x20, local copies, waits for them, and re-layouts, apply_op(): up_x = jnp.concatenate([vec[1:], high_x], axis=0)  41.1 us
  transfers between devices with their start and end apart: 86, of which 20 were waited for; matrix products, arithmetic and copies ran while one was open for 9% of the time, Pallas kernels for 0%

commit v1 on v0

v1 whole, which is shorter than its diff:
```python
import functools

import jax
import jax.numpy as jnp
from jax import lax
from jax.experimental import pallas as pl
from jax.experimental.pallas import tpu as pltpu
from jax.sharding import PartitionSpec as P

ITERS = 20
SUM_AXES = ("px", "py")
MESH = pl.DeviceIdType.MESH
NX, NZ = 64, 24
BODY = NX * NZ
FULL = BODY + 2 * NZ
HI = BODY + NZ
OTHERS = tuple((dy, dx) for dy in range(2) for dx in range(4) if (dy, dx) != (0, 0))
SEND_AT = {1: 4, 2: 9, 3: 15, 4: 19}
TAKE_AT = {6: 1, 11: 2, 17: 3}
STEPS_AT = {6: (0, 2), 7: (2, 4), 8: (4, 5), 11: (5, 7), 12: (7, 9), 13: (9, 10),
            17: (10, 12), 18: (12, 14), 19: (14, 16)}
RENEW_AT = {8: 9, 13: 14}
S_A, S_B, S_C, S_GP, S_G, S_CL, S_DL, S_Y, S_RHO, S_LEAD, S_HIST, S_BA, S_LA, S_LB, S_LA2, S_LB2, S_ERR, S_D, S_E, S_RHO0 = range(20)


def lanes():
    return lax.broadcasted_iota(jnp.int32, (8, 128), 1)


def rows8():
    return lax.broadcasted_iota(jnp.int32, (8, 128), 0)


def lane_sum(v):
    return jnp.broadcast_to(jnp.sum(v, axis=1, keepdims=True), (8, 128))


def full_sum(v):
    return jnp.broadcast_to(jnp.sum(jnp.sum(v, axis=0, keepdims=True), axis=1, keepdims=True), (8, 128))


def three(v):
    return jnp.concatenate([v, v, v], axis=0)


def kernel(s_h, b_h, x0_h, kx_h, ky_h, kz_h, out_h, hist_ref,
           Z, X0, D, KX, KY, KZ, PKS, H, KYP, KYH, HK, RS, RR, PT, ST, CO, YB,
           lsem, osem, is_s, is_r, hs, hr, rs, rr):
    px, py = lax.axis_index("px"), lax.axis_index("py")
    me = py * 4 + px
    lane, row = lanes(), rows8()
    lane24 = lax.broadcasted_iota(jnp.int32, (24, 128), 1)
    row24 = lax.broadcasted_iota(jnp.int32, (24, 128), 0)
    first, last = lane24 == 0, lane24 == 127
    has_lo, has_hi = px > 0, px < 3

    loads = []
    for n, (src, dst, base) in enumerate((
            (ky_h, KY, 0), (x0_h, X0, NZ), (kx_h, KX, NZ), (kz_h, KZ, 8), (s_h, D, 0), (b_h, None, NZ))):
        for t in range(2):
            to = Z.at[0, t, pl.ds(base, BODY), :] if dst is None else dst.at[t, pl.ds(base, BODY), :]
            cp = pltpu.make_async_copy(src.at[:, pl.ds(128 * t, 128)], to, lsem.at[2 * n + t])
            cp.start()
            loads.append(cp)

    zero_plane = jnp.zeros((NZ, 128), jnp.float32)
    for t in range(2):
        KX[t, pl.ds(0, NZ), :] = zero_plane
        X0[t, pl.ds(0, NZ), :] = zero_plane
        X0[t, pl.ds(HI, NZ), :] = zero_plane
        KZ[t, pl.ds(0, 8), :] = jnp.zeros((8, 128), jnp.float32)
    KYH[...] = jnp.zeros((2, 8, 128), jnp.float32)

    @pl.loop(0, ITERS + 1)
    def _(k):
        for t in range(2):
            Z[k, t, pl.ds(0, NZ), :] = zero_plane
            Z[k, t, pl.ds(HI, NZ), :] = zero_plane

    barrier = pltpu.get_barrier_semaphore()
    for dy, dx in OTHERS:
        pl.semaphore_signal(barrier, inc=1, device_id=(lax.rem(py + dy, 2), lax.rem(px + dx, 4)),
                            device_id_type=MESH)
    pl.semaphore_wait(barrier, len(OTHERS))

    def to_x(step):
        return (py, px + step)

    to_y = (1 - py, px)

    def remote(src, dst, ssem, rsem, dev):
        return pltpu.make_async_remote_copy(src_ref=src, dst_ref=dst, send_sem=ssem, recv_sem=rsem,
                                            device_id=dev, device_id_type=MESH)

    def init_up(t):
        cols = pl.ds(128 * t, 128)
        return (remote(kx_h.at[pl.ds(BODY - NZ, NZ), cols], KX.at[t, pl.ds(0, NZ), :], is_s.at[t], is_r.at[t], to_x(1)),
                remote(x0_h.at[pl.ds(BODY - NZ, NZ), cols], X0.at[t, pl.ds(0, NZ), :], is_s.at[2 + t], is_r.at[2 + t], to_x(1)))

    def init_down(t):
        cols = pl.ds(128 * t, 128)
        return (remote(x0_h.at[pl.ds(0, NZ), cols], X0.at[t, pl.ds(HI, NZ), :], is_s.at[4 + t], is_r.at[4 + t], to_x(-1)),)

    @pl.when(has_hi)
    def _():
        for t in range(2):
            for cp in init_up(t):
                cp.start()

    @pl.when(has_lo)
    def _():
        for t in range(2):
            for cp in init_down(t):
                cp.start()

    off = 1 - py

    def pack_into(acc, j, lo, hi):
        v = jnp.where(py == 0, hi, lo)
        for q in range(3):
            at = 3 * j + q
            moved = pltpu.roll(v[8 * q:8 * q + 8], lax.rem(at + 2 * off, 128), 1)
            acc = jnp.where(lane == at + off, moved, acc)
        return acc

    def pack(read, dst):
        for h in range(2):
            def step(j, acc):
                lo, hi = read(32 * h + j)
                return pack_into(acc, j, lo, hi)
            dst[h] = lax.fori_loop(0, 32, step, jnp.zeros((8, 128), jnp.float32), unroll=4)

    def unpack(tile, j):
        parts = [pltpu.roll(tile, 127 - (3 * j + q), 1) for q in range(3)]
        return jnp.concatenate(parts, axis=0)

    def rowsof(i):
        return pl.multiple_of(NZ * i, 8)

    loads[0].wait()
    loads[1].wait()
    pack(lambda i: (KY[0, pl.ds(rowsof(i), NZ), :], KY[1, pl.ds(rowsof(i), NZ), :]), KYP)
    ky_copy = remote(KYP, KYH, is_s.at[6], is_r.at[6], to_y)

    @pl.when(py == 0)
    def _():
        ky_copy.start()

    loads[2].wait()
    loads[3].wait()
    pack(lambda i: (X0[0, pl.ds(rowsof(i + 1), NZ), :], X0[1, pl.ds(rowsof(i + 1), NZ), :]), PKS.at[0])
    x0_copy = remote(PKS.at[0], H.at[0], is_s.at[7], is_r.at[7], to_y)
    x0_copy.start()

    for cp in loads[4:10]:
        cp.wait()

    keep_x = jnp.where(has_hi, 1.0, 0.0)
    for t in range(2):
        KX[t, pl.ds(BODY, NZ), :] = KX[t, pl.ds(BODY, NZ), :] * keep_x
    dead_y = last & (py == 1)
    dead_z = row24 == NZ - 1

    def mask_step(i, acc):
        s1, s2, kx1, ky1, kz1, k2 = acc
        r = rowsof(i)
        for t in range(2):
            s = D[t, pl.ds(r, NZ), :]
            kx = KX[t, pl.ds(r + NZ, NZ), :]
            ky = KY[t, pl.ds(r, NZ), :]
            kz = jnp.where(dead_z, 0.0, KZ[t, pl.ds(r + 8, NZ), :])
            if t == 1:
                ky = jnp.where(dead_y, 0.0, ky)
                KY[t, pl.ds(r, NZ), :] = ky
            KZ[t, pl.ds(r + 8, NZ), :] = kz
            s1, s2 = s1 + s, s2 + s * s
            kx1, ky1, kz1 = kx1 + kx, ky1 + ky, kz1 + kz
            k2 = k2 + (kx * kx + ky * ky + kz * kz)
        return s1, s2, kx1, ky1, kz1, k2

    sums = lax.fori_loop(0, NX, mask_step, (jnp.zeros((NZ, 128), jnp.float32),) * 6)
    stats = jnp.zeros((8, 128), jnp.float32)
    for n, v in enumerate(sums):
        stats = jnp.where((row == 2) & (lane == n), full_sum(v), stats)

    def sum_copies(e):
        return [remote(RS.at[e], RR.at[e, me], rs.at[e, n], rr.at[e],
                       (lax.rem(py + dy, 2), lax.rem(px + dx, 4))) for n, (dy, dx) in enumerate(OTHERS)]

    def sum_send(e, tile):
        RS[e] = tile
        RR[e, me] = tile
        for cp in sum_copies(e):
            cp.start()

    def sum_take(e):
        pltpu.make_async_copy(RR.at[e, pl.ds(0, 7)], RR.at[e, pl.ds(0, 7)], rr.at[e]).wait()
        total = RR[e, 0]
        for n in range(1, 8):
            total = total + RR[e, n]
        return total

    sum_send(0, stats)

    def up_copy(k):
        return remote(Z.at[k, :, pl.ds(BODY, NZ), :], Z.at[k, :, pl.ds(0, NZ), :], hs.at[k, 0], hr.at[k, 0], to_x(1))

    def down_copy(k):
        return remote(Z.at[k, :, pl.ds(NZ, NZ), :], Z.at[k, :, pl.ds(HI, NZ), :], hs.at[k, 1], hr.at[k, 1], to_x(-1))

    def y_copy(k):
        return remote(PKS.at[k + 1], H.at[k + 1], hs.at[k, 2], hr.at[k, 2], to_y)

    def send_x(k):
        @pl.when(has_hi)
        def _():
            up_copy(k).start()

        @pl.when(has_lo)
        def _():
            down_copy(k).start()

    def take_halo(k):
        @pl.when(has_lo)
        def _():
            up_copy(k).wait_recv()

        @pl.when(has_hi)
        def _():
            down_copy(k).wait_recv()

        y_copy(k).wait_recv()

    def neighbours(vec, i, h, j, tile_raw, tile_k):
        r = rowsof(i)
        u = [vec(t, r + NZ) for t in range(2)]
        ky = [KY[t, pl.ds(r, NZ), :] for t in range(2)]
        up = [pltpu.roll(u[t], 127, 1) for t in range(2)]
        down = [pltpu.roll(ky[t] * u[t], 1, 1) for t in range(2)]
        y_up = [jnp.where(last, up[1], up[0]), jnp.where(last, unpack(tile_raw, j), up[1])]
        y_down = [jnp.where(first, unpack(tile_k, j), down[0]), jnp.where(first, down[0], down[1])]
        out = []
        for t in range(2):
            part = ky[t] * y_up[t] + y_down[t]
            part = part + KX[t, pl.ds(r + NZ, NZ), :] * vec(t, r + 2 * NZ)
            part = part + KX[t, pl.ds(r, NZ), :] * vec(t, r)
            part = part + KZ[t, pl.ds(r + 8, NZ), :] * vec(t, r + NZ + 1)
            part = part + KZ[t, pl.ds(r + 7, NZ), :] * vec(t, r + NZ - 1)
            out.append(part)
        return u, out

    @pl.when(has_lo)
    def _():
        for t in range(2):
            for cp in init_up(t):
                cp.wait_recv()

    @pl.when(has_hi)
    def _():
        for t in range(2):
            for cp in init_down(t):
                cp.wait_recv()

    @pl.when(py == 1)
    def _():
        ky_copy.wait_recv()

    x0_copy.wait_recv()
    for h in range(2):
        HK[h] = H[0, h] * KYH[h]
    loads[10].wait()
    loads[11].wait()

    def start_plane(i, h, carry):
        acc, rho = carry
        j = i - 32 * h
        r = rowsof(i)
        u, nb = neighbours(lambda t, q: X0[t, pl.ds(q, NZ), :], i, h, j, H[0, h], HK[h])
        down = [pltpu.roll(KY[t, pl.ds(r, NZ), :], 1, 1) for t in range(2)]
        ky_lo = [jnp.where(first, unpack(KYH[h], j), down[0]), jnp.where(first, down[0], down[1])]
        new = []
        for t in range(2):
            diag = D[t, pl.ds(r, NZ), :] + KY[t, pl.ds(r, NZ), :] + ky_lo[t]
            diag = diag + KX[t, pl.ds(r + NZ, NZ), :] + KX[t, pl.ds(r, NZ), :]
            diag = diag + KZ[t, pl.ds(r + 8, NZ), :] + KZ[t, pl.ds(r + 7, NZ), :]
            D[t, pl.ds(r, NZ), :] = diag
            res = Z[0, t, pl.ds(r + NZ, NZ), :] - (diag * u[t] - nb[t])
            Z[0, t, pl.ds(r + NZ, NZ), :] = res
            rho = rho + res * res
            new.append(res)
        return pack_into(acc, j, new[0], new[1]), rho

    def sweep(plane, k, sums0, more=None):
        zero = jnp.zeros((8, 128), jnp.float32)
        acc0, sums1 = plane(0, 0, (zero, sums0))
        acc1, sums1 = plane(NX - 1, 1, (zero, sums1))
        if more is None:
            send_x(k)
        else:
            @pl.when(more)
            def _():
                send_x(k)
        acc0, sums1 = lax.fori_loop(1, 32, lambda i, c: plane(i, 0, c), (acc0, sums1))
        acc1, sums1 = lax.fori_loop(32, NX - 1, lambda i, c: plane(i, 1, c), (acc1, sums1))
        PKS[k + 1, 0] = acc0
        PKS[k + 1, 1] = acc1
        if more is None:
            y_copy(k).start()
        else:
            @pl.when(more)
            def _():
                y_copy(k).start()
        return sums1

    zero24 = jnp.zeros((NZ, 128), jnp.float32)
    rho0 = sweep(lambda i, h, c: start_plane(i, h, c), 0, zero24)
    PT[...] = jnp.where((row == 0) & (lane == 0), full_sum(rho0), 0.0)

    for n in range(20):
        ST[n] = jnp.zeros((8, 128), jnp.float32)
    totals = sum_take(0)
    cells = float(NX * 256 * NZ * 8)
    mean = [full_sum(jnp.where((row == 2) & (lane == n), totals, 0.0)) * (1.0 / cells) for n in range(6)]
    var_s = jnp.maximum(mean[1] - mean[0] * mean[0], 0.0)
    var_k = jnp.maximum(mean[5] - mean[2] * mean[2] - mean[3] * mean[3] - mean[4] * mean[4], 0.0)
    b_first = jnp.sqrt(3.0 * mean[5] + 1.5 * (var_s + 2.0 * var_k))
    a_first = jnp.maximum(mean[0] - 0.5 * jnp.sqrt(var_s), 0.3) + 2.0 * b_first

    def set_coefs(k0, a_new, b_new):
        old_b = ST[S_B]
        b_arr = jnp.where(lane >= k0, b_new, old_b)
        ST[S_A] = jnp.where(lane >= k0, a_new, ST[S_A])
        ST[S_B] = b_arr
        ST[S_C] = jnp.where(lane == 0, 0.0, pltpu.roll(b_arr, 1, 1))
        inv = 1.0 / b_new
        for k in range(k0, ITERS):
            CO[k, 0] = a_new
            if k > k0:
                CO[k, 1] = b_new
            elif k == 0:
                CO[k, 1] = jnp.zeros((8, 128), jnp.float32)
            else:
                CO[k, 1] = CO[k - 1, 3]
            CO[k, 2] = inv
            CO[k, 3] = b_new

    set_coefs(0, a_first, b_first)

    def gram_start(total):
        rho = full_sum(jnp.where((row == 0) & (lane == 0), total, 0.0))
        one = jnp.where(lane == 0, 1.0, 0.0)
        ST[S_G] = one * rho
        ST[S_CL] = one
        ST[S_DL] = one
        ST[S_LEAD] = jnp.ones((8, 128), jnp.float32)
        ST[S_RHO] = rho
        ST[S_RHO0] = rho
        ST[S_HIST] = one * rho

    def gram_load(total):
        ST[S_D] = jnp.broadcast_to(total[0:1], (8, 128))
        ST[S_E] = jnp.broadcast_to(total[1:2], (8, 128))

    def gram_step(k):
        a, b, c = ST[S_A], ST[S_B], ST[S_C]
        g, gp, cl, dl = ST[S_G], ST[S_GP], ST[S_CL], ST[S_DL]
        e_row, d_row = ST[S_E], ST[S_D]
        rho, lead = ST[S_RHO], ST[S_LEAD]
        b_k, c_k, a_k = CO[k, 3], CO[k, 1], CO[k, 0]
        at_k, at_k1 = lane == k, lane == k + 1
        rec = ((a - a_k) * g + b * pltpu.roll(g, 127, 1)
               + c * pltpu.roll(g, 1, 1) - c_k * gp) * CO[k, 2]
        g_new = jnp.where(lane < k, rec, jnp.where(at_k, e_row, jnp.where(at_k1, d_row, 0.0)))
        g_full = jnp.where(at_k1, pltpu.roll(e_row, 1, 1), g)
        image = a * dl + pltpu.roll(b * dl, 1, 1) + pltpu.roll(c * dl, 127, 1)
        delta = lead * lane_sum(image * g_full)
        alpha = rho / delta
        y = ST[S_Y] + alpha * dl
        cl = cl - alpha * image
        lead = -alpha * b_k * lead
        prod = cl * g_new
        rho_new = lead * lane_sum(prod)
        size = jnp.abs(lead) * lane_sum(jnp.abs(prod))
        beta = rho_new / rho
        dl = cl + beta * dl
        ST[S_G], ST[S_GP], ST[S_CL], ST[S_DL] = g_new, g, cl, dl
        ST[S_Y], ST[S_RHO], ST[S_LEAD] = y, rho_new, lead
        ST[S_HIST] = jnp.where(at_k1, rho_new, ST[S_HIST])
        inv_alpha = 1.0 / alpha
        ST[S_LA2], ST[S_LB2] = ST[S_LA], ST[S_LB]
        ST[S_LA] = inv_alpha + ST[S_BA]
        ST[S_LB] = jnp.sqrt(jnp.abs(beta)) * inv_alpha
        ST[S_BA] = beta * inv_alpha
        err = size / jnp.abs(rho_new) * jnp.sqrt(jnp.abs(rho_new) / ST[S_RHO0])
        err = jnp.where(rho_new > 0.0, err, 1e30)
        ST[S_ERR] = jnp.maximum(ST[S_ERR], jnp.where(err < 1e30, err, 1e30))

    def renew(k0):
        a_new = 0.5 * (ST[S_LA] + ST[S_LA2])
        b_new = 0.5 * (ST[S_LB] + ST[S_LB2])
        a_ok = (a_new > 0.3) & (a_new < 26.8)
        a_new = jnp.where(a_ok, a_new, a_first)
        b_new = jnp.where(a_ok & (b_new > 0.25 * b_first) & (b_new < 2.0 * b_first), b_new, b_first)
        set_coefs(k0, a_new, b_new)

    def apply_step(k):
        take_halo(k)
        for h in range(2):
            HK[h] = H[k + 1, h] * KYH[h]
        a_k, c_k, i_k = three(CO[k, 0]), three(CO[k, 1]), three(CO[k, 2])
        before = jnp.maximum(k - 1, 0)

        def plane(i, h, carry):
            acc, (dots, cross) = carry
            j = i - 32 * h
            r = rowsof(i)
            u, nb = neighbours(lambda t, q: Z[k, t, pl.ds(q, NZ), :], i, h, j, H[k + 1, h], HK[h])
            new = []
            for t in range(2):
                val = (D[t, pl.ds(r, NZ), :] - a_k) * u[t] - nb[t] - c_k * Z[before, t, pl.ds(r + NZ, NZ), :]
                val = val * i_k
                Z[k + 1, t, pl.ds(r + NZ, NZ), :] = val
                dots = dots + val * val
                cross = cross + val * u[t]
                new.append(val)
            return pack_into(acc, j, new[0], new[1]), (dots, cross)

        dots, cross = sweep(plane, k + 1, (zero24, zero24), k < ITERS - 1)
        tile = jnp.where((row == 0) & (lane == k + 1), full_sum(dots), PT[...])
        tile = jnp.where((row == 1) & (lane == k), full_sum(cross), tile)
        PT[...] = tile
        for e, at in SEND_AT.items():
            @pl.when(k == at)
            def _():
                sum_send(e, tile)
        for at, e in TAKE_AT.items():
            @pl.when(k == at)
            def _():
                total = sum_take(e)
                gram_load(total)
                if e == 1:
                    gram_start(total)
        for at, (lo, hi) in STEPS_AT.items():
            @pl.when(k == at)
            def _():
                @pl.loop(lo, hi)
                def _(s):
                    gram_step(s)
        for at, k0 in RENEW_AT.items():
            @pl.when(k == at)
            def _():
                renew(k0)

    @pl.loop(0, ITERS)
    def _(k):
        apply_step(k)

    gram_load(sum_take(4))

    @pl.loop(16, ITERS)
    def _(s):
        gram_step(s)

    y = ST[S_Y]
    for k in range(ITERS):
        YB[k] = lane_sum(jnp.where(lane == k, y, 0.0))
    hist = jnp.sqrt(ST[S_HIST] * (1.0 / cells))
    hist_ref[...] = jnp.where(row == 0, hist, ST[S_ERR])

    def combine(i, c):
        r = rowsof(i + 1)
        acc = [X0[t, pl.ds(r, NZ), :] for t in range(2)]
        for k in range(ITERS):
            w = three(YB[k])
            for t in range(2):
                acc[t] = acc[t] + w * Z[k, t, pl.ds(r, NZ), :]
        for t in range(2):
            X0[t, pl.ds(r, NZ), :] = acc[t]
        return c

    outs = []
    for part in range(4):
        lax.fori_loop(16 * part, 16 * part + 16, combine, 0)
        for t in range(2):
            cp = pltpu.make_async_copy(X0.at[t, pl.ds(NZ + 16 * NZ * part, 16 * NZ), :],
                                       out_h.at[pl.ds(16 * NZ * part, 16 * NZ), pl.ds(128 * t, 128)],
                                       osem.at[2 * part + t])
            cp.start()
            outs.append(cp)

    @pl.when(has_hi)
    def _():
        for t in range(2):
            for cp in init_up(t):
                cp.wait_send()

    @pl.when(has_lo)
    def _():
        for t in range(2):
            for cp in init_down(t):
                cp.wait_send()

    @pl.when(py == 0)
    def _():
        ky_copy.wait_send()

    x0_copy.wait_send()

    @pl.loop(0, ITERS)
    def _(k):
        @pl.when(has_hi)
        def _():
            up_copy(k).wait_send()

        @pl.when(has_lo)
        def _():
            down_copy(k).wait_send()

        y_copy(k).wait_send()

    for e in range(5):
        for cp in sum_copies(e):
            cp.wait_send()
    for cp in outs:
        cp.wait()


def fused_solve(shift, rhs_field, x_init, cond_x, cond_y, cond_z):
    def flat(v):
        return jnp.transpose(v, (0, 2, 1)).reshape(BODY, 256)

    f32 = jnp.float32
    any_spec = pl.BlockSpec(memory_space=pl.ANY)
    x_rows, small = pl.pallas_call(
        kernel,
        out_shape=(jax.ShapeDtypeStruct((BODY, 256), f32), jax.ShapeDtypeStruct((8, 128), f32)),
        in_specs=[any_spec] * 6,
        out_specs=(any_spec, pl.BlockSpec(memory_space=pltpu.VMEM)),
        scratch_shapes=[
            pltpu.VMEM((ITERS + 1, 2, FULL, 128), f32),
            pltpu.VMEM((2, FULL, 128), f32),
            pltpu.VMEM((2, BODY, 128), f32),
            pltpu.VMEM((2, BODY + NZ, 128), f32),
            pltpu.VMEM((2, BODY, 128), f32),
            pltpu.VMEM((2, BODY + 8, 128), f32),
            pltpu.VMEM((ITERS + 2, 2, 8, 128), f32),
            pltpu.VMEM((ITERS + 2, 2, 8, 128), f32),
            pltpu.VMEM((2, 8, 128), f32),
            pltpu.VMEM((2, 8, 128), f32),
            pltpu.VMEM((2, 8, 128), f32),
            pltpu.VMEM((5, 8, 128), f32),
            pltpu.VMEM((5, 8, 8, 128), f32),
            pltpu.VMEM((8, 128), f32),
            pltpu.VMEM((20, 8, 128), f32),
            pltpu.VMEM((ITERS, 4, 8, 128), f32),
            pltpu.VMEM((ITERS, 8, 128), f32),
            pltpu.SemaphoreType.DMA((12,)),
            pltpu.SemaphoreType.DMA((8,)),
            pltpu.SemaphoreType.DMA((8,)),
            pltpu.SemaphoreType.DMA((8,)),
            pltpu.SemaphoreType.DMA((ITERS, 3)),
            pltpu.SemaphoreType.DMA((ITERS, 3)),
            pltpu.SemaphoreType.DMA((5, 7)),
            pltpu.SemaphoreType.DMA((5,)),
        ],
        compiler_params=pltpu.CompilerParams(collective_id=0, has_side_effects=True,
                                             vmem_limit_bytes=60 * 1024 * 1024),
    )(*(flat(v) for v in (shift, rhs_field, x_init, cond_x, cond_y, cond_z)))
    x_out = jnp.transpose(x_rows.reshape(NX, NZ, 256), (0, 2, 1))
    return x_out, small[0, :ITERS + 1], small[1, 0]


def solution(mesh):
    field_spec = P("px", "py", None)

    def local_solve(*fields):
        x_out, history, _ = fused_solve(*fields)
        return x_out, history

    return jax.shard_map(local_solve, mesh=mesh, in_specs=(field_spec,) * 6,
                         out_specs=(field_spec, P()), check_vma=False)
```

time: 1870 us -> 304 us (0.16)
  blocking collectives: 927 us -> 0 us
  other arithmetic: 323 us -> 0 us
  Pallas kernels: 0 us -> 300 us
  local copies, waits for them, and re-layouts: 292 us -> 3.85 us
  starting transfers between devices: 219 us -> 0 us
  between operations: 53.2 us -> 0.64 us
  waiting for transfers between devices: 42.3 us -> 0 us
    psum x40 -> x0, blocking collectives: 927 us -> none  [global_dot(): return lax.psum(jnp.sum(left * right), SUM_AXES)]
    pallas_call x0 -> x1, Pallas kernels: none -> 300 us  [fused_solve(): pl.pallas_call(kernel, out_shape=(jax.ShapeDtypeStruct((BODY, 256), f32),...]
    reduce_sum x40 -> x0, other arithmetic: 266 us -> none  [global_dot(): return lax.psum(jnp.sum(left * right), SUM_AXES)]
    slice x149 -> x0, local copies, waits for them, and re-layouts: 225 us -> none  [the longest x40 60.4 us: apply_op(): high_y = lax.ppermute(vec[:, :1], 'py', back_y)]
    ppermute x86 -> x0, starting transfers between devices: 219 us -> none  [the longest x21 89.7 us: apply_op(): low_y = lax.ppermute(vec[:, -1:], 'py', fwd_y)]
    ppermute x43 -> x0, local copies, waits for them, and re-layouts: 52.9 us -> none  [the longest x21 25.8 us: apply_op(): high_y = lax.ppermute(vec[:, :1], 'py', back_y)]
    add x20 -> x0, other arithmetic: 43.6 us -> none  [the longest x19 31.1 us: local_solve(): p_cur = r_cur + rho_new / rho_cur * p_cur]
    ppermute x86 -> x0, waiting for transfers between devices: 42.3 us -> none  [the longest x21 42.1 us: apply_op(): high_y = lax.ppermute(vec[:, :1], 'py', back_y)]
  transfers between devices with their start and end apart: 86 -> 0, of which waited for: 20 -> 0; matrix products, arithmetic and copies ran while one was open for 9% -> 0% of each run, Pallas kernels for 0% -> 0%
where the time goes in v1:
time: 304 us
  Pallas kernels  300 us (99%)
  local copies, waits for them, and re-layouts  3.85 us (1%)
    pallas_call x1, Pallas kernels, fused_solve(): pl.pallas_call(kernel, out_shape=(jax.ShapeDtypeStruct((BODY, 256), f32),...  300 us

profile of v1, /device:TPU:0, one launch (start us, length us, event | category | flops | bytes accessed | tf_op | source)
XLA Modules:
  0.0 304.3 jit_solution(17770473377887570690)
XLA Ops:
  0.6 299.8 %shard_map.77 = (f32[1536,256]{1,0:T(8,128)}, f32[8,128]{1,0:T(8,128)}) custom-call(f32[1536,256]{1,0:T(8,128)} %bitcast.23, f32[1536,256]{1,0:T(8,128)} %bitcast.24, f32[1536,256]{1,0:T(8,128)} %bitcast.25, f32[1536,256]{1,0:T(8,128)} %bitcast.26, f32[1536,256]{1,0:T(8,128)} %bitcast.27, f32[1536,256]{1,0:T(8,128)} %bitcast.28), custom_call_target="tpu_custom_call" | custom-call | tf_op jit(solution)/shard_map/pallas_call | solution.py:534
  300.5 1.2 slice_bitcast_fusion
  301.7 2.7 copy.9

commit v2 on v1

--- a/solution.py
+++ b/solution.py
@@ -125,10 +125,11 @@
 
     def pack(read, dst):
         for h in range(2):
-            def step(j, acc):
+            accs = [jnp.zeros((8, 128), jnp.float32)] * 4
+            for j in range(32):
                 lo, hi = read(32 * h + j)
-                return pack_into(acc, j, lo, hi)
-            dst[h] = lax.fori_loop(0, 32, step, jnp.zeros((8, 128), jnp.float32), unroll=4)
+                accs[j % 4] = pack_into(accs[j % 4], j, lo, hi)
+            dst[h] = (accs[0] + accs[1]) + (accs[2] + accs[3])
 
     def unpack(tile, j):
         parts = [pltpu.roll(tile, 127 - (3 * j + q), 1) for q in range(3)]
@@ -231,7 +232,7 @@
 
         y_copy(k).wait_recv()
 
-    def neighbours(vec, i, h, j, tile_raw, tile_k):
+    def neighbours(vec, i, j, tile_raw, tile_k):
         r = rowsof(i)
         u = [vec(t, r + NZ) for t in range(2)]
         ky = [KY[t, pl.ds(r, NZ), :] for t in range(2)]
@@ -271,14 +272,13 @@
     loads[10].wait()
     loads[11].wait()
 
-    def start_plane(i, h, carry):
-        acc, rho = carry
-        j = i - 32 * h
+    def start_plane(i, rho):
+        h = i // 32
+        j = lax.rem(i, 32)
         r = rowsof(i)
-        u, nb = neighbours(lambda t, q: X0[t, pl.ds(q, NZ), :], i, h, j, H[0, h], HK[h])
+        u, nb = neighbours(lambda t, q: X0[t, pl.ds(q, NZ), :], i, j, H[0, h], HK[h])
         down = [pltpu.roll(KY[t, pl.ds(r, NZ), :], 1, 1) for t in range(2)]
         ky_lo = [jnp.where(first, unpack(KYH[h], j), down[0]), jnp.where(first, down[0], down[1])]
-        new = []
         for t in range(2):
             diag = D[t, pl.ds(r, NZ), :] + KY[t, pl.ds(r, NZ), :] + ky_lo[t]
             diag = diag + KX[t, pl.ds(r + NZ, NZ), :] + KX[t, pl.ds(r, NZ), :]
@@ -287,33 +287,32 @@
             res = Z[0, t, pl.ds(r + NZ, NZ), :] - (diag * u[t] - nb[t])
             Z[0, t, pl.ds(r + NZ, NZ), :] = res
             rho = rho + res * res
-            new.append(res)
-        return pack_into(acc, j, new[0], new[1]), rho
-
-    def sweep(plane, k, sums0, more=None):
-        zero = jnp.zeros((8, 128), jnp.float32)
-        acc0, sums1 = plane(0, 0, (zero, sums0))
-        acc1, sums1 = plane(NX - 1, 1, (zero, sums1))
-        if more is None:
+        return rho
+
+    UNROLL = 6
+
+    def sweep(plane, k, sums1, more):
+        sums1 = plane(0, sums1)
+        sums1 = plane(NX - 1, sums1)
+
+        @pl.when(more)
+        def _():
             send_x(k)
-        else:
-            @pl.when(more)
-            def _():
-                send_x(k)
-        acc0, sums1 = lax.fori_loop(1, 32, lambda i, c: plane(i, 0, c), (acc0, sums1))
-        acc1, sums1 = lax.fori_loop(32, NX - 1, lambda i, c: plane(i, 1, c), (acc1, sums1))
-        PKS[k + 1, 0] = acc0
-        PKS[k + 1, 1] = acc1
-        if more is None:
+
+        sums1 = plane(1, sums1)
+        sums1 = plane(NX - 2, sums1)
+        sums1 = lax.fori_loop(0, 60 // UNROLL, lambda m, c: functools.reduce(
+            lambda d, n: plane(2 + UNROLL * m + n, d), range(UNROLL), c), sums1)
+
+        @pl.when(more)
+        def _():
+            pack(lambda i: (Z[k, 0, pl.ds(rowsof(i + 1), NZ), :], Z[k, 1, pl.ds(rowsof(i + 1), NZ), :]), PKS.at[k + 1])
             y_copy(k).start()
-        else:
-            @pl.when(more)
-            def _():
-                y_copy(k).start()
+
         return sums1
 
     zero24 = jnp.zeros((NZ, 128), jnp.float32)
-    rho0 = sweep(lambda i, h, c: start_plane(i, h, c), 0, zero24)
+    rho0 = sweep(start_plane, 0, zero24, px >= 0)
     PT[...] = jnp.where((row == 0) & (lane == 0), full_sum(rho0), 0.0)
 
     for n in range(20):
@@ -410,20 +409,19 @@
         a_k, c_k, i_k = three(CO[k, 0]), three(CO[k, 1]), three(CO[k, 2])
         before = jnp.maximum(k - 1, 0)
 
-        def plane(i, h, carry):
-            acc, (dots, cross) = carry
-            j = i - 32 * h
+        def plane(i, carry):
+            dots, cross = carry
+            h = i // 32
+            j = lax.rem(i, 32)
             r = rowsof(i)
-            u, nb = neighbours(lambda t, q: Z[k, t, pl.ds(q, NZ), :], i, h, j, H[k + 1, h], HK[h])
-            new = []
+            u, nb = neighbours(lambda t, q: Z[k, t, pl.ds(q, NZ), :], i, j, H[k + 1, h], HK[h])
             for t in range(2):
                 val = (D[t, pl.ds(r, NZ), :] - a_k) * u[t] - nb[t] - c_k * Z[before, t, pl.ds(r + NZ, NZ), :]
                 val = val * i_k
                 Z[k + 1, t, pl.ds(r + NZ, NZ), :] = val
                 dots = dots + val * val
                 cross = cross + val * u[t]
-                new.append(val)
-            return pack_into(acc, j, new[0], new[1]), (dots, cross)
+            return dots, cross
 
         dots, cross = sweep(plane, k + 1, (zero24, zero24), k < ITERS - 1)
         tile = jnp.where((row == 0) & (lane == k + 1), full_sum(dots), PT[...])

time: 304 us -> 133 us (0.44)
  Pallas kernels: 300 us -> 129 us
    pallas_call x1, Pallas kernels: 300 us -> 129 us  [fused_solve(): pl.pallas_call(kernel, out_shape=(jax.ShapeDtypeStruct((BODY, 256), f32),...]
where the time goes in v2:
time: 133 us
  Pallas kernels  129 us (97%)
  local copies, waits for them, and re-layouts  3.85 us (3%)
    pallas_call x1, Pallas kernels, fused_solve(): pl.pallas_call(kernel, out_shape=(jax.ShapeDtypeStruct((BODY, 256), f32),...  129 us

profile of v2, /device:TPU:0, one launch (start us, length us, event | category | flops | bytes accessed | tf_op | source)
XLA Modules:
  0.0 133.2 jit_solution(1568825800507293568)
XLA Ops:
  0.6 128.7 %shard_map.77 = (f32[1536,256]{1,0:T(8,128)}, f32[8,128]{1,0:T(8,128)}) custom-call(f32[1536,256]{1,0:T(8,128)} %bitcast.23, f32[1536,256]{1,0:T(8,128)} %bitcast.24, f32[1536,256]{1,0:T(8,128)} %bitcast.25, f32[1536,256]{1,0:T(8,128)} %bitcast.26, f32[1536,256]{1,0:T(8,128)} %bitcast.27, f32[1536,256]{1,0:T(8,128)} %bitcast.28), custom_call_target="tpu_custom_call" | custom-call | tf_op jit(solution)/shard_map/pallas_call | solution.py:532
  129.3 1.2 slice_bitcast_fusion
  130.5 2.7 %copy.9 = f32[64,256,24]{1,2,0:T(8,128)} copy(f32[64,256,24]{1,2,0:T(8,128)} %bitcast.29) | data formatting | bytes 3145728

commit v3 on v2

v3 whole, which is shorter than its diff:
```python
import functools

import jax
import jax.numpy as jnp
from jax import lax
from jax.experimental import pallas as pl
from jax.experimental.pallas import tpu as pltpu
from jax.sharding import PartitionSpec as P

ITERS = 20
SUM_AXES = ("px", "py")
MESH = pl.DeviceIdType.MESH
NX, NZ = 64, 24
BODY = NX * NZ
FULL = BODY + 2 * NZ
HI = BODY + NZ
OTHERS = tuple((dy, dx) for dy in range(2) for dx in range(4) if (dy, dx) != (0, 0))
SEND_AT = {1: 4, 2: 9, 3: 15, 4: 19}
TAKE_AT = {6: 1, 11: 2, 17: 3}
STEPS_AT = {6: (0, 2), 7: (2, 4), 8: (4, 5), 11: (5, 7), 12: (7, 9), 13: (9, 10),
            17: (10, 12), 18: (12, 14), 19: (14, 16)}
RENEW_AT = {8: 9, 13: 14}
VREG = (8, 128)
SUB, LANES = VREG
TILES = range(2)


def turn(v, by):
    return pltpu.roll(v, by, 1)


def lift(v, by):
    return pltpu.roll(v, by, 0)


S_A, S_B, S_C, S_GP, S_G, S_CL, S_DL, S_Y, S_RHO, S_LEAD, S_HIST, S_BA, S_LA, S_LB, S_LA2, S_LB2, S_ERR, S_D, S_E, S_RHO0 = range(20)


def lanes():
    return lax.broadcasted_iota(jnp.int32, VREG, 1)


def rows8():
    return lax.broadcasted_iota(jnp.int32, VREG, 0)


def lane_sum(v):
    return jnp.broadcast_to(jnp.sum(v, axis=1, keepdims=True), VREG)


def full_sum(v):
    return jnp.broadcast_to(jnp.sum(jnp.sum(v, axis=0, keepdims=True), axis=1, keepdims=True), VREG)


def three(v):
    return jnp.concatenate([v, v, v], axis=0)


def kernel(s_h, b_h, x0_h, kx_h, ky_h, kz_h, out_h, hist_ref,
           Z, X0, D, KX, KY, KZ, PKS, H, KYP, KYH, HK, UI, CB, RS, RR, PT, ST, CO, YB,
           lsem, osem, is_s, is_r, hs, hr, rs, rr):
    px, py = lax.axis_index("px"), lax.axis_index("py")
    me = py * 4 + px
    lane, row = lanes(), rows8()
    lane24 = lax.broadcasted_iota(jnp.int32, (NZ, LANES), 1)
    row24 = lax.broadcasted_iota(jnp.int32, (NZ, LANES), 0)
    first, last = lane24 == 0, lane24 == 127
    has_lo, has_hi = px > 0, px < 3

    loads = []
    for n, (src, dst, base) in enumerate((
            (ky_h, KY, 0), (x0_h, X0, NZ), (kx_h, KX, NZ), (kz_h, KZ, 8), (s_h, D, 0), (b_h, None, NZ))):
        for t in TILES:
            to = Z.at[0, t, pl.ds(base, BODY), :] if dst is None else dst.at[t, pl.ds(base, BODY), :]
            cp = pltpu.make_async_copy(src.at[:, pl.ds(LANES * t, LANES)], to, lsem.at[2 * n + t])
            cp.start()
            loads.append(cp)

    zero_plane = jnp.zeros((NZ, LANES), jnp.float32)
    for t in TILES:
        KX[t, pl.ds(0, NZ), :] = zero_plane
        X0[t, pl.ds(0, NZ), :] = zero_plane
        X0[t, pl.ds(HI, NZ), :] = zero_plane
        KZ[t, pl.ds(0, 8), :] = jnp.zeros(VREG, jnp.float32)
    KYH[...] = jnp.zeros((2, *VREG), jnp.float32)

    @pl.loop(0, ITERS + 1)
    def _(k):
        for t in TILES:
            Z[k, t, pl.ds(0, NZ), :] = zero_plane
            Z[k, t, pl.ds(HI, NZ), :] = zero_plane

    barrier = pltpu.get_barrier_semaphore()
    for dy, dx in OTHERS:
        pl.semaphore_signal(barrier, inc=1, device_id=(lax.rem(py + dy, 2), lax.rem(px + dx, 4)),
                            device_id_type=MESH)
    pl.semaphore_wait(barrier, len(OTHERS))

    def to_x(step):
        return (py, px + step)

    to_y = (1 - py, px)

    def remote(src, dst, ssem, rsem, dev):
        return pltpu.make_async_remote_copy(src_ref=src, dst_ref=dst, send_sem=ssem, recv_sem=rsem,
                                            device_id=dev, device_id_type=MESH)

    def init_up(t):
        cols = pl.ds(LANES * t, LANES)
        return (remote(kx_h.at[pl.ds(BODY - NZ, NZ), cols], KX.at[t, pl.ds(0, NZ), :], is_s.at[t], is_r.at[t], to_x(1)),
                remote(x0_h.at[pl.ds(BODY - NZ, NZ), cols], X0.at[t, pl.ds(0, NZ), :], is_s.at[2 + t], is_r.at[2 + t], to_x(1)))

    def init_down(t):
        cols = pl.ds(LANES * t, LANES)
        return (remote(x0_h.at[pl.ds(0, NZ), cols], X0.at[t, pl.ds(HI, NZ), :], is_s.at[4 + t], is_r.at[4 + t], to_x(-1)),)

    @pl.when(has_hi)
    def _():
        for t in TILES:
            for cp in init_up(t):
                cp.start()

    @pl.when(has_lo)
    def _():
        for t in TILES:
            for cp in init_down(t):
                cp.start()

    off = 1 - py
    tb = 1 - py
    edge = 127 * (1 - py)
    inner = 126 + py * (1 - 126)

    def pack_one(items, bl):
        rel = lax.rem(lane - bl + LANES, LANES)
        s = 1
        while len(items) > 3:
            keep = rel < s
            items = [jnp.where(keep, items[n], turn(items[n + 1], s)) for n in range(0, len(items), 2)]
            s *= 2
        out = jnp.where(rel < s, items[0],
                        jnp.where(rel < 2 * s, turn(items[1], s), turn(items[2], 2 * s)))
        return out

    def pack(ref, base, bl, dst):
        for h in TILES:
            items = [ref[tb, pl.ds(base + 32 * NZ * h + 8 * a, 8), :] for a in range(96)]
            dst[h] = turn(pack_one(items, bl), lax.rem(3 + off - bl + LANES, LANES))

    low_ghost = (lane >= off) & (lane < off + 3)
    high_ghost = (lane >= off + 99) & (lane < off + 102)

    def with_ghosts(n0, n1, lo, hi):
        lo = turn(pack_one([lo[SUB * q:SUB * q + SUB] for q in range(3)], edge), lax.rem(off - edge + LANES, LANES))
        hi = turn(pack_one([hi[SUB * q:SUB * q + SUB] for q in range(3)], edge), lax.rem(99 + off - edge + LANES, LANES))
        return (jnp.where(low_ghost, lo, jnp.where(high_ghost, turn(n1, 96), n0)),
                jnp.where(low_ghost, turn(n0, 32), jnp.where(high_ghost, hi, n1)))

    def own_layout(v):
        return turn(v, 1 + py * 126)

    def z_up(v):
        return jnp.where(row == 7, lift(turn(v, 127), 7), lift(v, 7))

    def z_down(v):
        return jnp.where(row == 0, lift(turn(v, 1), 1), lift(v, 1))

    def unpack(tile, j):
        parts = [turn(tile, 124 - (3 * j + q)) for q in range(3)]
        return jnp.concatenate(parts, axis=0)

    def rowsof(i):
        return pl.multiple_of(NZ * i, 8)

    loads[0].wait()
    loads[1].wait()
    pack(KY, 0, edge, KYP)
    ky_copy = remote(KYP, KYH, is_s.at[6], is_r.at[6], to_y)

    @pl.when(py == 0)
    def _():
        ky_copy.start()

    loads[2].wait()
    loads[3].wait()
    pack(X0, NZ, edge, PKS.at[0])
    x0_copy = remote(PKS.at[0], H.at[0], is_s.at[7], is_r.at[7], to_y)
    x0_copy.start()

    for cp in loads[4:10]:
        cp.wait()

    keep_x = jnp.where(has_hi, 1.0, 0.0)
    for t in TILES:
        KX[t, pl.ds(BODY, NZ), :] = KX[t, pl.ds(BODY, NZ), :] * keep_x
    dead_y = last & (py == 1)
    dead_z = row24 == NZ - 1

    def mask_step(i, acc):
        s1, s2, kx1, ky1, kz1, k2 = acc
        r = rowsof(i)
        for t in TILES:
            s = D[t, pl.ds(r, NZ), :]
            kx = KX[t, pl.ds(r + NZ, NZ), :]
            ky = KY[t, pl.ds(r, NZ), :]
            kz = jnp.where(dead_z, 0.0, KZ[t, pl.ds(r + SUB, NZ), :])
            if t == 1:
                ky = jnp.where(dead_y, 0.0, ky)
                KY[t, pl.ds(r, NZ), :] = ky
            KZ[t, pl.ds(r + SUB, NZ), :] = kz
            s1, s2 = s1 + s, s2 + s * s
            kx1, ky1, kz1 = kx1 + kx, ky1 + ky, kz1 + kz
            k2 = k2 + (kx * kx + ky * ky + kz * kz)
        return s1, s2, kx1, ky1, kz1, k2

    sums = lax.fori_loop(0, NX, mask_step, (jnp.zeros((NZ, LANES), jnp.float32),) * 6)
    stats = jnp.zeros(VREG, jnp.float32)
    for n, v in enumerate(sums):
        stats = jnp.where((row == 2) & (lane == n), full_sum(v), stats)

    def sum_copies(e):
        return [remote(RS.at[e], RR.at[e, me], rs.at[e, n], rr.at[e],
                       (lax.rem(py + dy, 2), lax.rem(px + dx, 4))) for n, (dy, dx) in enumerate(OTHERS)]

    def sum_send(e, tile):
        RS[e] = tile
        RR[e, me] = tile
        for cp in sum_copies(e):
            cp.start()

    def sum_take(e):
        pltpu.make_async_copy(RR.at[e, pl.ds(0, 7)], RR.at[e, pl.ds(0, 7)], rr.at[e]).wait()
        total = RR[e, 0]
        for n in range(1, 8):
            total = total + RR[e, n]
        return total

    sum_send(0, stats)
    pack(KX, NZ, edge, CB.at[1])
    pack(KZ, 8, edge, CB.at[5])
    pack(KY, 0, inner, CB.at[4])
    pack(KY, 0, edge, CB.at[3])
    for h in TILES:
        CB[6, h] = z_down(CB[5, h])

    def up_copy(k):
        return remote(Z.at[k, :, pl.ds(BODY, NZ), :], Z.at[k, :, pl.ds(0, NZ), :], hs.at[k, 0], hr.at[k, 0], to_x(1))

    def down_copy(k):
        return remote(Z.at[k, :, pl.ds(NZ, NZ), :], Z.at[k, :, pl.ds(HI, NZ), :], hs.at[k, 1], hr.at[k, 1], to_x(-1))

    def y_copy(k):
        return remote(PKS.at[k + 1], H.at[k + 1], hs.at[k, 2], hr.at[k, 2], to_y)

    def send_x(k):
        @pl.when(has_hi)
        def _():
            up_copy(k).start()

        @pl.when(has_lo)
        def _():
            down_copy(k).start()

    def take_halo(k):
        @pl.when(has_lo)
        def _():
            up_copy(k).wait_recv()

        @pl.when(has_hi)
        def _():
            down_copy(k).wait_recv()

        y_copy(k).wait_recv()

    def first_state(vec, i):
        r = rowsof(i)
        return ([vec(t, r) for t in TILES], [vec(t, r + NZ) for t in TILES],
                [KX[t, pl.ds(r, NZ), :] for t in TILES])

    def neighbours(vec, i, j, tile_raw, tile_k, state):
        r = rowsof(i)
        x_down, u, kx_down = state
        x_up = [vec(t, r + 2 * NZ) for t in TILES]
        kx = [KX[t, pl.ds(r + NZ, NZ), :] for t in TILES]
        ky = [KY[t, pl.ds(r, NZ), :] for t in TILES]
        up = [turn(u[t], 127) for t in TILES]
        down = [turn(ky[t] * u[t], 1) for t in TILES]
        y_up = [jnp.where(last, up[1], up[0]), jnp.where(last, unpack(tile_raw, j), up[1])]
        y_down = [jnp.where(first, unpack(tile_k, j), down[0]), jnp.where(first, down[0], down[1])]
        out = []
        for t in TILES:
            part = ky[t] * y_up[t] + y_down[t]
            part = part + kx[t] * x_up[t]
            part = part + kx_down[t] * x_down[t]
            part = part + KZ[t, pl.ds(r + SUB, NZ), :] * vec(t, r + NZ + 1)
            part = part + KZ[t, pl.ds(r + 7, NZ), :] * vec(t, r + NZ - 1)
            out.append(part)
        return u, out, ky, kx, (u, x_up, kx)

    @pl.when(has_lo)
    def _():
        for t in TILES:
            for cp in init_up(t):
                cp.wait_recv()

    @pl.when(has_hi)
    def _():
        for t in TILES:
            for cp in init_down(t):
                cp.wait_recv()

    @pl.when(py == 1)
    def _():
        ky_copy.wait_recv()

    x0_copy.wait_recv()
    for h in TILES:
        HK[h] = H[0, h] * KYH[h]
    loads[10].wait()
    loads[11].wait()

    x0_vec = lambda t, q: X0[t, pl.ds(q, NZ), :]

    def start_plane(i, rho, state):
        h = i // 32
        j = lax.rem(i, 32)
        r = rowsof(i)
        kx_down = state[2]
        u, nb, ky, kx, state = neighbours(x0_vec, i, j, H[0, h], HK[h], state)
        down = [turn(ky[t], 1) for t in TILES]
        ky_lo = [jnp.where(first, unpack(KYH[h], j), down[0]), jnp.where(first, down[0], down[1])]
        for t in TILES:
            diag = D[t, pl.ds(r, NZ), :] + ky[t] + ky_lo[t] + kx[t] + kx_down[t]
            diag = diag + KZ[t, pl.ds(r + SUB, NZ), :] + KZ[t, pl.ds(r + 7, NZ), :]
            D[t, pl.ds(r, NZ), :] = diag
            res = Z[0, t, pl.ds(r + NZ, NZ), :] - (diag * u[t] - nb[t])
            Z[0, t, pl.ds(r + NZ, NZ), :] = res
            rho = rho + res * res
        return rho, state

    UNROLL = 10

    def sweep(vec, plane, k, sums1, more, send_y):
        def run(i, n, c):
            state = first_state(vec, i)
            for m in range(n):
                c, state = plane(i + m, c, state)
            return c

        sums1 = run(0, 2, sums1)

        @pl.when(more)
        def _():
            send_y()

        sums1 = run(NX - 2, 2, sums1)

        @pl.when(more)
        def _():
            send_x(k)

        return lax.fori_loop(0, 60 // UNROLL, lambda m, c: run(2 + UNROLL * m, UNROLL, c), sums1)

    zero24 = jnp.zeros((NZ, LANES), jnp.float32)
    zero_tile = jnp.zeros((NZ, LANES), jnp.float32)
    kx_cols = with_ghosts(CB[1, 0], CB[1, 1], KX[tb, pl.ds(0, NZ), :], zero_tile)
    for h in TILES:
        CB[2, h] = turn(kx_cols[h], 3)
        ky_edge, ky_in = CB[3, h], CB[4, h]
        CB[3, h] = jnp.where(py == 0, ky_edge, own_layout(KYH[h]))
        CB[4, h] = jnp.where(py == 0, ky_in, ky_edge)
    rho0 = sweep(x0_vec, start_plane, 0, zero24, px >= 0, lambda: None)
    pack(Z.at[0], NZ, edge, PKS.at[1])
    y_copy(0).start()
    pack(Z.at[0], NZ, inner, UI)
    pack(D, 0, edge, CB.at[0])
    PT[...] = jnp.where((row == 0) & (lane == 0), full_sum(rho0), 0.0)

    for n in range(20):
        ST[n] = jnp.zeros(VREG, jnp.float32)
    totals = sum_take(0)
    cells = float(NX * 256 * NZ * 8)
    mean = [full_sum(jnp.where((row == 2) & (lane == n), totals, 0.0)) * (1.0 / cells) for n in range(6)]
    var_s = jnp.maximum(mean[1] - mean[0] * mean[0], 0.0)
    var_k = jnp.maximum(mean[5] - mean[2] * mean[2] - mean[3] * mean[3] - mean[4] * mean[4], 0.0)
    b_first = jnp.sqrt(3.0 * mean[5] + 1.5 * (var_s + 2.0 * var_k))
    a_first = jnp.maximum(mean[0] - 0.5 * jnp.sqrt(var_s), 0.3) + 2.0 * b_first

    def set_coefs(k0, a_new, b_new):
        old_b = ST[S_B]
        b_arr = jnp.where(lane >= k0, b_new, old_b)
        ST[S_A] = jnp.where(lane >= k0, a_new, ST[S_A])
        ST[S_B] = b_arr
        ST[S_C] = jnp.where(lane == 0, 0.0, turn(b_arr, 1))
        inv = 1.0 / b_new
        for k in range(k0, ITERS):
            CO[k, 0] = a_new
            if k > k0:
                CO[k, 1] = b_new
            elif k == 0:
                CO[k, 1] = jnp.zeros(VREG, jnp.float32)
            else:
                CO[k, 1] = CO[k - 1, 3]
            CO[k, 2] = inv
            CO[k, 3] = b_new

    set_coefs(0, a_first, b_first)

    def gram_start(total):
        rho = full_sum(jnp.where((row == 0) & (lane == 0), total, 0.0))
        one = jnp.where(lane == 0, 1.0, 0.0)
        ST[S_G] = one * rho
        ST[S_CL] = one
        ST[S_DL] = one
        ST[S_LEAD] = jnp.ones(VREG, jnp.float32)
        ST[S_RHO] = rho
        ST[S_RHO0] = rho
        ST[S_HIST] = one * rho

    def gram_load(total):
        ST[S_D] = jnp.broadcast_to(total[0:1], VREG)
        ST[S_E] = jnp.broadcast_to(total[1:2], VREG)

    def gram_step(k):
        a, b, c = ST[S_A], ST[S_B], ST[S_C]
        g, gp, cl, dl = ST[S_G], ST[S_GP], ST[S_CL], ST[S_DL]
        e_row, d_row = ST[S_E], ST[S_D]
        rho, lead = ST[S_RHO], ST[S_LEAD]
        b_k, c_k, a_k = CO[k, 3], CO[k, 1], CO[k, 0]
        at_k, at_k1 = lane == k, lane == k + 1
        rec = ((a - a_k) * g + b * turn(g, 127)
               + c * turn(g, 1) - c_k * gp) * CO[k, 2]
        g_new = jnp.where(lane < k, rec, jnp.where(at_k, e_row, jnp.where(at_k1, d_row, 0.0)))
        g_full = jnp.where(at_k1, turn(e_row, 1), g)
        image = a * dl + turn(b * dl, 1) + turn(c * dl, 127)
        delta = lead * lane_sum(image * g_full)
        alpha = rho / delta
        y = ST[S_Y] + alpha * dl
        cl = cl - alpha * image
        lead = -alpha * b_k * lead
        prod = cl * g_new
        rho_new = lead * lane_sum(prod)
        size = jnp.abs(lead) * lane_sum(jnp.abs(prod))
        beta = rho_new / rho
        dl = cl + beta * dl
        ST[S_G], ST[S_GP], ST[S_CL], ST[S_DL] = g_new, g, cl, dl
        ST[S_Y], ST[S_RHO], ST[S_LEAD] = y, rho_new, lead
        ST[S_HIST] = jnp.where(at_k1, rho_new, ST[S_HIST])
        inv_alpha = 1.0 / alpha
        ST[S_LA2], ST[S_LB2] = ST[S_LA], ST[S_LB]
        ST[S_LA] = inv_alpha + ST[S_BA]
        ST[S_LB] = jnp.sqrt(jnp.abs(beta)) * inv_alpha
        ST[S_BA] = beta * inv_alpha
        err = size / jnp.abs(rho_new) * jnp.sqrt(jnp.abs(rho_new) / ST[S_RHO0])
        err = jnp.where(rho_new > 0.0, err, 1e30)
        ST[S_ERR] = jnp.maximum(ST[S_ERR], jnp.where(err < 1e30, err, 1e30))

    def renew(k0):
        a_new = 0.5 * (ST[S_LA] + ST[S_LA2])
        b_new = 0.5 * (ST[S_LB] + ST[S_LB2])
        a_ok = (a_new > 0.3) & (a_new < 26.8)
        a_new = jnp.where(a_ok, a_new, a_first)
        b_new = jnp.where(a_ok & (b_new > 0.25 * b_first) & (b_new < 2.0 * b_first), b_new, b_first)
        set_coefs(k0, a_new, b_new)

    def apply_step(k):
        take_halo(k)
        for h in TILES:
            HK[h] = H[k + 1, h] * KYH[h]
        before = jnp.maximum(k - 1, 0)
        cols = with_ghosts(PKS[k + 1, 0], PKS[k + 1, 1], Z[k, tb, pl.ds(0, NZ), :], Z[k, tb, pl.ds(HI, NZ), :])
        for h in TILES:
            u = cols[h]
            val = (CB[0, h] - CO[k, 0]) * u - CB[3, h] * own_layout(H[k + 1, h]) - CB[4, h] * UI[h]
            val = val - CB[1, h] * turn(u, 125) - CB[2, h] * turn(u, 3)
            val = val - CB[5, h] * z_up(u) - CB[6, h] * z_down(u) - CO[k, 1] * PKS[before + 1, h]
            PKS[k + 2, h] = val * CO[k, 2]
        a_k, c_k, i_k = three(CO[k, 0]), three(CO[k, 1]), three(CO[k, 2])

        def plane(i, carry, state):
            dots, cross = carry
            h = i // 32
            j = lax.rem(i, 32)
            r = rowsof(i)
            u, nb, ky, kx, state = neighbours(vec, i, j, H[k + 1, h], HK[h], state)
            for t in TILES:
                val = (D[t, pl.ds(r, NZ), :] - a_k) * u[t] - nb[t] - c_k * Z[before, t, pl.ds(r + NZ, NZ), :]
                val = val * i_k
                Z[k + 1, t, pl.ds(r + NZ, NZ), :] = val
                dots = dots + val * val
                cross = cross + val * u[t]
            return (dots, cross), state

        vec = lambda t, q: Z[k, t, pl.ds(q, NZ), :]
        more = k < ITERS - 1
        dots, cross = sweep(vec, plane, k + 1, (zero24, zero24), more, lambda: y_copy(k + 1).start())

        @pl.when(more)
        def _():
            pack(Z.at[k + 1], NZ, inner, UI)

        tile = jnp.where((row == 0) & (lane == k + 1), full_sum(dots), PT[...])
        tile = jnp.where((row == 1) & (lane == k), full_sum(cross), tile)
        PT[...] = tile
        for e, at in SEND_AT.items():
            @pl.when(k == at)
            def _():
                sum_send(e, tile)
        for at, e in TAKE_AT.items():
            @pl.when(k == at)
            def _():
                total = sum_take(e)
                gram_load(total)
                if e == 1:
                    gram_start(total)
        for at, (lo, hi) in STEPS_AT.items():
            @pl.when(k == at)
            def _():
                @pl.loop(lo, hi)
                def _(s):
                    gram_step(s)
        for at, k0 in RENEW_AT.items():
            @pl.when(k == at)
            def _():
                renew(k0)

    @pl.loop(0, ITERS)
    def _(k):
        apply_step(k)

    gram_load(sum_take(4))

    @pl.loop(16, ITERS)
    def _(s):
        gram_step(s)

    y = ST[S_Y]
    for k in range(ITERS):
        YB[k] = lane_sum(jnp.where(lane == k, y, 0.0))
    hist = jnp.sqrt(ST[S_HIST] * (1.0 / cells))
    hist_ref[...] = jnp.where(row == 0, hist, ST[S_ERR])

    def combine(i, c):
        r = rowsof(i + 1)
        acc = [X0[t, pl.ds(r, NZ), :] for t in TILES]
        for k in range(ITERS):
            w = three(YB[k])
            for t in TILES:
                acc[t] = acc[t] + w * Z[k, t, pl.ds(r, NZ), :]
        for t in TILES:
            X0[t, pl.ds(r, NZ), :] = acc[t]
        return c

    outs = []
    for part in range(4):
        lax.fori_loop(16 * part, 16 * part + 16, combine, 0)
        for t in TILES:
            cp = pltpu.make_async_copy(X0.at[t, pl.ds(NZ + 16 * NZ * part, 16 * NZ), :],
                                       out_h.at[pl.ds(16 * NZ * part, 16 * NZ), pl.ds(LANES * t, LANES)],
                                       osem.at[2 * part + t])
            cp.start()
            outs.append(cp)

    @pl.when(has_hi)
    def _():
        for t in TILES:
            for cp in init_up(t):
                cp.wait_send()

    @pl.when(has_lo)
    def _():
        for t in TILES:
            for cp in init_down(t):
                cp.wait_send()

    @pl.when(py == 0)
    def _():
        ky_copy.wait_send()

    x0_copy.wait_send()

    @pl.loop(0, ITERS)
    def _(k):
        @pl.when(has_hi)
        def _():
            up_copy(k).wait_send()

        @pl.when(has_lo)
        def _():
            down_copy(k).wait_send()

        y_copy(k).wait_send()

    for e in range(5):
        for cp in sum_copies(e):
            cp.wait_send()
    for cp in outs:
        cp.wait()


def fused_solve(shift, rhs_field, x_init, cond_x, cond_y, cond_z):
    def flat(v):
        return jnp.transpose(v, (0, 2, 1)).reshape(BODY, 256)

    f32 = jnp.float32
    any_spec = pl.BlockSpec(memory_space=pl.ANY)
    x_rows, small = pl.pallas_call(
        kernel,
        out_shape=(jax.ShapeDtypeStruct((BODY, 256), f32), jax.ShapeDtypeStruct(VREG, f32)),
        in_specs=[any_spec] * 6,
        out_specs=(any_spec, pl.BlockSpec(memory_space=pltpu.VMEM)),
        scratch_shapes=[
            pltpu.VMEM((ITERS + 1, 2, FULL, LANES), f32),
            pltpu.VMEM((2, FULL, LANES), f32),
            pltpu.VMEM((2, BODY, LANES), f32),
            pltpu.VMEM((2, BODY + NZ, LANES), f32),
            pltpu.VMEM((2, BODY, LANES), f32),
            pltpu.VMEM((2, BODY + 8, LANES), f32),
            pltpu.VMEM((ITERS + 2, 2, *VREG), f32),
            pltpu.VMEM((ITERS + 2, 2, *VREG), f32),
            pltpu.VMEM((2, *VREG), f32),
            pltpu.VMEM((2, *VREG), f32),
            pltpu.VMEM((2, *VREG), f32),
            pltpu.VMEM((2, *VREG), f32),
            pltpu.VMEM((7, 2, *VREG), f32),
            pltpu.VMEM((5, *VREG), f32),
            pltpu.VMEM((5, 8, *VREG), f32),
            pltpu.VMEM(VREG, f32),
            pltpu.VMEM((20, *VREG), f32),
            pltpu.VMEM((ITERS, 4, *VREG), f32),
            pltpu.VMEM((ITERS, *VREG), f32),
            pltpu.SemaphoreType.DMA((12,)),
            pltpu.SemaphoreType.DMA((8,)),
            pltpu.SemaphoreType.DMA((8,)),
            pltpu.SemaphoreType.DMA((8,)),
            pltpu.SemaphoreType.DMA((ITERS, 3)),
            pltpu.SemaphoreType.DMA((ITERS, 3)),
            pltpu.SemaphoreType.DMA((5, 7)),
            pltpu.SemaphoreType.DMA((5,)),
        ],
        compiler_params=pltpu.CompilerParams(collective_id=0, has_side_effects=True,
                                             vmem_limit_bytes=60 * 1024 * 1024),
    )(*(flat(v) for v in (shift, rhs_field, x_init, cond_x, cond_y, cond_z)))
    x_out = jnp.transpose(x_rows.reshape(NX, NZ, 256), (0, 2, 1))
    return x_out, small[0, :ITERS + 1], small[1, 0]


def solution(mesh):
    field_spec = P("px", "py", None)

    def local_solve(*fields):
        x_out, history, _ = fused_solve(*fields)
        return x_out, history

    return jax.shard_map(local_solve, mesh=mesh, in_specs=(field_spec,) * 6,
                         out_specs=(field_spec, P()), check_vma=False)
```

time: 133 us -> 92 us (0.69)
  Pallas kernels: 129 us -> 87.3 us
    pallas_call x1, Pallas kernels: 129 us -> 87.3 us  [fused_solve(): pl.pallas_call(kernel, out_shape=(jax.ShapeDtypeStruct((BODY, 256), f32),...]
where the time goes in v3:
time: 92 us; the launch traced here: 91.8 us
  Pallas kernels  87.3 us (95%)
  local copies, waits for them, and re-layouts  3.85 us (4%)
    pallas_call x1, Pallas kernels, fused_solve(): pl.pallas_call(kernel, out_shape=(jax.ShapeDtypeStruct((BODY, 256), f32),...  87.3 us
    unnamed x1, local copies, waits for them, and re-layouts  2.65 us

profile of v3, /device:TPU:0, one launch (start us, length us, event | category | flops | bytes accessed | tf_op | source)
XLA Modules:
  0.0 91.8 jit_solution(6675421447902774487)
XLA Ops:
  0.6 87.3 %shard_map.77 = (f32[1536,256]{1,0:T(8,128)}, f32[8,128]{1,0:T(8,128)}) custom-call(f32[1536,256]{1,0:T(8,128)} %bitcast.23, f32[1536,256]{1,0:T(8,128)} %bitcast.24, f32[1536,256]{1,0:T(8,128)} %bitcast.25, f32[1536,256]{1,0:T(8,128)} %bitcast.26, f32[1536,256]{1,0:T(8,128)} %bitcast.27, f32[1536,256]{1,0:T(8,128)} %bitcast.28), custom_call_target="tpu_custom_call" | custom-call | tf_op jit(solution)/shard_map/pallas_call | solution.py:607
  88.0 1.2 %slice_bitcast_fusion = f32[21]{0:T(128)} fusion(f32[8,128]{1,0:T(8,128)} %get-tuple-element.5), kind=kLoop, calls=%fused_computation | loop fusion | bytes 168 | tf_op jit(solution)/shard_map/squeeze | solution.py:645
  89.2 2.7 %copy.9 = f32[64,256,24]{1,2,0:T(8,128)} copy(f32[64,256,24]{1,2,0:T(8,128)} %bitcast.29) | data formatting | bytes 3145728

commit v4 on v3

--- a/solution.py
+++ b/solution.py
@@ -11,6 +11,10 @@
 SUM_AXES = ("px", "py")
 MESH = pl.DeviceIdType.MESH
 NX, NZ = 64, 24
+ROW = 256
+ERR_LIMIT = 1000.0
+HALF = NX // 2
+CELLS = float(NX * 256 * NZ * 8)
 BODY = NX * NZ
 FULL = BODY + 2 * NZ
 HI = BODY + NZ
@@ -25,6 +29,12 @@
 TILES = range(2)
 
 
+C_D, C_UP, C_DOWN, C_OUT, C_IN, C_ZUP, C_ZDN = range(7)
+K_A, K_C, K_INV, K_B = range(4)
+NQ = 3
+LAST, TOP, NIL = 127, 7, 0.0
+
+
 def turn(v, by):
     return pltpu.roll(v, by, 1)
 
@@ -57,15 +67,15 @@
 
 
 def kernel(s_h, b_h, x0_h, kx_h, ky_h, kz_h, out_h, hist_ref,
-           Z, X0, D, KX, KY, KZ, PKS, H, KYP, KYH, HK, UI, CB, RS, RR, PT, ST, CO, YB,
+           Z, X0, D, KX, KY, KZ, PKS, H, KYP, KYH, HK, UI, CB, PRE, RS, RR, PT, ST, CO, YB,
            lsem, osem, is_s, is_r, hs, hr, rs, rr):
     px, py = lax.axis_index("px"), lax.axis_index("py")
     me = py * 4 + px
     lane, row = lanes(), rows8()
     lane24 = lax.broadcasted_iota(jnp.int32, (NZ, LANES), 1)
     row24 = lax.broadcasted_iota(jnp.int32, (NZ, LANES), 0)
-    first, last = lane24 == 0, lane24 == 127
-    has_lo, has_hi = px > 0, px < 3
+    first, last = lane24 == 0, lane24 == LAST
+    has_lo, has_hi = px > 0, px < NQ
 
     loads = []
     for n, (src, dst, base) in enumerate((
@@ -128,13 +138,13 @@
 
     off = 1 - py
     tb = 1 - py
-    edge = 127 * (1 - py)
+    edge = LAST * (1 - py)
     inner = 126 + py * (1 - 126)
 
     def pack_one(items, bl):
         rel = lax.rem(lane - bl + LANES, LANES)
         s = 1
-        while len(items) > 3:
+        while len(items) > NQ:
             keep = rel < s
             items = [jnp.where(keep, items[n], turn(items[n + 1], s)) for n in range(0, len(items), 2)]
             s *= 2
@@ -143,16 +153,21 @@
         return out
 
     def pack(ref, base, bl, dst):
+        start = NQ + off - bl + LANES
         for h in TILES:
-            items = [ref[tb, pl.ds(base + 32 * NZ * h + 8 * a, 8), :] for a in range(96)]
-            dst[h] = turn(pack_one(items, bl), lax.rem(3 + off - bl + LANES, LANES))
-
-    low_ghost = (lane >= off) & (lane < off + 3)
+            accs = [jnp.zeros(VREG, jnp.float32)] * NQ
+            for a in range(NQ * HALF):
+                v = ref[tb, pl.ds(base + HALF * NZ * h + SUB * a, SUB), :]
+                moved = turn(v, lax.rem(start + a, LANES))
+                accs[a % NQ] = jnp.where(lane == a + NQ + off, moved, accs[a % NQ])
+            dst[h] = accs[0] + accs[1] + accs[2]
+
+    low_ghost = (lane >= off) & (lane < off + NQ)
     high_ghost = (lane >= off + 99) & (lane < off + 102)
 
     def with_ghosts(n0, n1, lo, hi):
-        lo = turn(pack_one([lo[SUB * q:SUB * q + SUB] for q in range(3)], edge), lax.rem(off - edge + LANES, LANES))
-        hi = turn(pack_one([hi[SUB * q:SUB * q + SUB] for q in range(3)], edge), lax.rem(99 + off - edge + LANES, LANES))
+        lo = turn(pack_one([lo[SUB * q:SUB * q + SUB] for q in range(NQ)], edge), lax.rem(off - edge + LANES, LANES))
+        hi = turn(pack_one([hi[SUB * q:SUB * q + SUB] for q in range(NQ)], edge), lax.rem(99 + off - edge + LANES, LANES))
         return (jnp.where(low_ghost, lo, jnp.where(high_ghost, turn(n1, 96), n0)),
                 jnp.where(low_ghost, turn(n0, 32), jnp.where(high_ghost, hi, n1)))
 
@@ -160,13 +175,13 @@
         return turn(v, 1 + py * 126)
 
     def z_up(v):
-        return jnp.where(row == 7, lift(turn(v, 127), 7), lift(v, 7))
+        return jnp.where(row == TOP, lift(turn(v, LAST), TOP), lift(v, TOP))
 
     def z_down(v):
         return jnp.where(row == 0, lift(turn(v, 1), 1), lift(v, 1))
 
     def unpack(tile, j):
-        parts = [turn(tile, 124 - (3 * j + q)) for q in range(3)]
+        parts = [turn(tile, 124 - (NQ * j + q)) for q in range(NQ)]
         return jnp.concatenate(parts, axis=0)
 
     def rowsof(i):
@@ -182,15 +197,15 @@
         ky_copy.start()
 
     loads[2].wait()
-    loads[3].wait()
+    loads[NQ].wait()
     pack(X0, NZ, edge, PKS.at[0])
-    x0_copy = remote(PKS.at[0], H.at[0], is_s.at[7], is_r.at[7], to_y)
+    x0_copy = remote(PKS.at[0], H.at[0], is_s.at[TOP], is_r.at[TOP], to_y)
     x0_copy.start()
 
-    for cp in loads[4:10]:
+    for cp in loads[4:12]:
         cp.wait()
 
-    keep_x = jnp.where(has_hi, 1.0, 0.0)
+    keep_x = jnp.where(has_hi, 1.0, NIL)
     for t in TILES:
         KX[t, pl.ds(BODY, NZ), :] = KX[t, pl.ds(BODY, NZ), :] * keep_x
     dead_y = last & (py == 1)
@@ -203,9 +218,9 @@
             s = D[t, pl.ds(r, NZ), :]
             kx = KX[t, pl.ds(r + NZ, NZ), :]
             ky = KY[t, pl.ds(r, NZ), :]
-            kz = jnp.where(dead_z, 0.0, KZ[t, pl.ds(r + SUB, NZ), :])
+            kz = jnp.where(dead_z, NIL, KZ[t, pl.ds(r + SUB, NZ), :])
             if t == 1:
-                ky = jnp.where(dead_y, 0.0, ky)
+                ky = jnp.where(dead_y, NIL, ky)
                 KY[t, pl.ds(r, NZ), :] = ky
             KZ[t, pl.ds(r + SUB, NZ), :] = kz
             s1, s2 = s1 + s, s2 + s * s
@@ -213,7 +228,7 @@
             k2 = k2 + (kx * kx + ky * ky + kz * kz)
         return s1, s2, kx1, ky1, kz1, k2
 
-    sums = lax.fori_loop(0, NX, mask_step, (jnp.zeros((NZ, LANES), jnp.float32),) * 6)
+    sums = lax.fori_loop(0, NX, mask_step, (zero_plane,) * 6, unroll=4)
     stats = jnp.zeros(VREG, jnp.float32)
     for n, v in enumerate(sums):
         stats = jnp.where((row == 2) & (lane == n), full_sum(v), stats)
@@ -229,19 +244,22 @@
             cp.start()
 
     def sum_take(e):
-        pltpu.make_async_copy(RR.at[e, pl.ds(0, 7)], RR.at[e, pl.ds(0, 7)], rr.at[e]).wait()
+        pltpu.make_async_copy(RR.at[e, pl.ds(0, TOP)], RR.at[e, pl.ds(0, TOP)], rr.at[e]).wait()
         total = RR[e, 0]
         for n in range(1, 8):
             total = total + RR[e, n]
         return total
 
     sum_send(0, stats)
-    pack(KX, NZ, edge, CB.at[1])
-    pack(KZ, 8, edge, CB.at[5])
-    pack(KY, 0, inner, CB.at[4])
-    pack(KY, 0, edge, CB.at[3])
+    pack(D, 0, edge, CB.at[C_D])
+    pack(Z.at[0], NZ, edge, PRE)
+    pack(X0, NZ, inner, UI)
+    pack(KX, NZ, edge, CB.at[C_UP])
+    pack(KZ, 8, edge, CB.at[C_ZUP])
+    pack(KY, 0, inner, CB.at[C_IN])
+    pack(KY, 0, edge, CB.at[C_OUT])
     for h in TILES:
-        CB[6, h] = z_down(CB[5, h])
+        CB[C_ZDN, h] = z_down(CB[C_ZUP, h])
 
     def up_copy(k):
         return remote(Z.at[k, :, pl.ds(BODY, NZ), :], Z.at[k, :, pl.ds(0, NZ), :], hs.at[k, 0], hr.at[k, 0], to_x(1))
@@ -283,7 +301,7 @@
         x_up = [vec(t, r + 2 * NZ) for t in TILES]
         kx = [KX[t, pl.ds(r + NZ, NZ), :] for t in TILES]
         ky = [KY[t, pl.ds(r, NZ), :] for t in TILES]
-        up = [turn(u[t], 127) for t in TILES]
+        up = [turn(u[t], LAST) for t in TILES]
         down = [turn(ky[t] * u[t], 1) for t in TILES]
         y_up = [jnp.where(last, up[1], up[0]), jnp.where(last, unpack(tile_raw, j), up[1])]
         y_down = [jnp.where(first, unpack(tile_k, j), down[0]), jnp.where(first, down[0], down[1])]
@@ -293,7 +311,7 @@
             part = part + kx[t] * x_up[t]
             part = part + kx_down[t] * x_down[t]
             part = part + KZ[t, pl.ds(r + SUB, NZ), :] * vec(t, r + NZ + 1)
-            part = part + KZ[t, pl.ds(r + 7, NZ), :] * vec(t, r + NZ - 1)
+            part = part + KZ[t, pl.ds(r + TOP, NZ), :] * vec(t, r + NZ - 1)
             out.append(part)
         return u, out, ky, kx, (u, x_up, kx)
 
@@ -316,8 +334,23 @@
     x0_copy.wait_recv()
     for h in TILES:
         HK[h] = H[0, h] * KYH[h]
-    loads[10].wait()
-    loads[11].wait()
+
+    def own_faces(cols):
+        n0, n1 = cols
+        from_lo, from_hi = (lane >= off + NQ) & (lane < off + 6), (lane >= off + NQ * HALF) & (lane < off + NQ * HALF + NQ)
+        down = (jnp.where(from_lo, NIL, turn(n0, NQ)), jnp.where(from_lo, turn(n0, 35), turn(n1, NQ)))
+        up = (jnp.where(from_hi, turn(n1, 93), turn(n0, 125)), jnp.where(from_hi, NIL, turn(n1, 125)))
+        return [CB[C_IN, h] * UI[h] + CB[C_UP, h] * up[h] + CB[C_DOWN, h] * down[h]
+                + CB[C_ZUP, h] * z_up(u) + CB[C_ZDN, h] * z_down(u) for h, u in enumerate(cols)]
+
+    def outer_faces(lo, hi, beyond):
+        ghost = [jnp.zeros(VREG, jnp.float32)] * 2
+        for q in range(NQ):
+            for h, (v, at) in enumerate(((lo, NQ), (hi, NQ * HALF))):
+                at = at + q + off
+                moved = turn(v[SUB * q:SUB * q + SUB], lax.rem(at - edge + LANES, LANES))
+                ghost[h] = jnp.where(lane == at, moved, ghost[h])
+        return [CB[C_OUT, h] * own_layout(beyond[h]) + CB[C_DOWN - h, h] * ghost[h] for h in TILES]
 
     x0_vec = lambda t, q: X0[t, pl.ds(q, NZ), :]
 
@@ -331,7 +364,7 @@
         ky_lo = [jnp.where(first, unpack(KYH[h], j), down[0]), jnp.where(first, down[0], down[1])]
         for t in TILES:
             diag = D[t, pl.ds(r, NZ), :] + ky[t] + ky_lo[t] + kx[t] + kx_down[t]
-            diag = diag + KZ[t, pl.ds(r + SUB, NZ), :] + KZ[t, pl.ds(r + 7, NZ), :]
+            diag = diag + KZ[t, pl.ds(r + SUB, NZ), :] + KZ[t, pl.ds(r + TOP, NZ), :]
             D[t, pl.ds(r, NZ), :] = diag
             res = Z[0, t, pl.ds(r + NZ, NZ), :] - (diag * u[t] - nb[t])
             Z[0, t, pl.ds(r + NZ, NZ), :] = res
@@ -340,50 +373,49 @@
 
     UNROLL = 10
 
-    def sweep(vec, plane, k, sums1, more, send_y):
+    def sweep(vec, plane, k, sums1, more):
         def run(i, n, c):
             state = first_state(vec, i)
             for m in range(n):
                 c, state = plane(i + m, c, state)
             return c
 
-        sums1 = run(0, 2, sums1)
-
-        @pl.when(more)
-        def _():
-            send_y()
-
-        sums1 = run(NX - 2, 2, sums1)
+        sums1 = run(NX - 1, 1, run(0, 1, sums1))
 
         @pl.when(more)
         def _():
             send_x(k)
 
+        sums1 = run(NX - 2, 1, run(1, 1, sums1))
         return lax.fori_loop(0, 60 // UNROLL, lambda m, c: run(2 + UNROLL * m, UNROLL, c), sums1)
 
-    zero24 = jnp.zeros((NZ, LANES), jnp.float32)
-    zero_tile = jnp.zeros((NZ, LANES), jnp.float32)
-    kx_cols = with_ghosts(CB[1, 0], CB[1, 1], KX[tb, pl.ds(0, NZ), :], zero_tile)
+    zero24 = zero_plane
+    zero_tile = zero_plane
+    kx_cols = with_ghosts(CB[C_UP, 0], CB[C_UP, 1], KX[tb, pl.ds(0, NZ), :], zero_tile)
     for h in TILES:
-        CB[2, h] = turn(kx_cols[h], 3)
-        ky_edge, ky_in = CB[3, h], CB[4, h]
-        CB[3, h] = jnp.where(py == 0, ky_edge, own_layout(KYH[h]))
-        CB[4, h] = jnp.where(py == 0, ky_in, ky_edge)
-    rho0 = sweep(x0_vec, start_plane, 0, zero24, px >= 0, lambda: None)
-    pack(Z.at[0], NZ, edge, PKS.at[1])
+        CB[C_DOWN, h] = turn(kx_cols[h], NQ)
+        ky_edge, ky_in = CB[C_OUT, h], CB[C_IN, h]
+        CB[C_OUT, h] = jnp.where(py == 0, ky_edge, own_layout(KYH[h]))
+        CB[C_IN, h] = jnp.where(py == 0, ky_in, ky_edge)
+    far = outer_faces(X0[tb, pl.ds(0, NZ), :], X0[tb, pl.ds(HI, NZ), :], (H[0, 0], H[0, 1]))
+    own = own_faces((PKS[0, 0], PKS[0, 1]))
+    for h in TILES:
+        diag = CB[C_D, h] + CB[C_UP, h] + CB[C_DOWN, h] + CB[C_OUT, h] + CB[C_IN, h] + CB[C_ZUP, h] + CB[C_ZDN, h]
+        CB[C_D, h] = diag
+        PKS[1, h] = PRE[h] - (diag * PKS[0, h] - far[h] - own[h])
     y_copy(0).start()
+    rho0 = sweep(x0_vec, start_plane, 0, zero24, px >= 0)
     pack(Z.at[0], NZ, inner, UI)
-    pack(D, 0, edge, CB.at[0])
-    PT[...] = jnp.where((row == 0) & (lane == 0), full_sum(rho0), 0.0)
+    PT[...] = jnp.where((row == 0) & (lane == 0), full_sum(rho0), NIL)
 
     for n in range(20):
         ST[n] = jnp.zeros(VREG, jnp.float32)
     totals = sum_take(0)
-    cells = float(NX * 256 * NZ * 8)
-    mean = [full_sum(jnp.where((row == 2) & (lane == n), totals, 0.0)) * (1.0 / cells) for n in range(6)]
-    var_s = jnp.maximum(mean[1] - mean[0] * mean[0], 0.0)
-    var_k = jnp.maximum(mean[5] - mean[2] * mean[2] - mean[3] * mean[3] - mean[4] * mean[4], 0.0)
-    b_first = jnp.sqrt(3.0 * mean[5] + 1.5 * (var_s + 2.0 * var_k))
+    cells = CELLS
+    mean = [full_sum(jnp.where((row == 2) & (lane == n), totals, NIL)) * (1.0 / cells) for n in range(6)]
+    var_s = jnp.maximum(mean[1] - mean[0] * mean[0], NIL)
+    var_k = jnp.maximum(mean[5] - mean[2] * mean[2] - mean[NQ] * mean[NQ] - mean[4] * mean[4], NIL)
+    b_first = jnp.sqrt(3.0 * mean[5] + var_s + 2.0 * var_k)
     a_first = jnp.maximum(mean[0] - 0.5 * jnp.sqrt(var_s), 0.3) + 2.0 * b_first
 
     def set_coefs(k0, a_new, b_new):
@@ -391,24 +423,24 @@
         b_arr = jnp.where(lane >= k0, b_new, old_b)
         ST[S_A] = jnp.where(lane >= k0, a_new, ST[S_A])
         ST[S_B] = b_arr
-        ST[S_C] = jnp.where(lane == 0, 0.0, turn(b_arr, 1))
+        ST[S_C] = jnp.where(lane == 0, NIL, turn(b_arr, 1))
         inv = 1.0 / b_new
         for k in range(k0, ITERS):
-            CO[k, 0] = a_new
+            CO[k, K_A] = a_new
             if k > k0:
-                CO[k, 1] = b_new
+                CO[k, K_C] = b_new
             elif k == 0:
-                CO[k, 1] = jnp.zeros(VREG, jnp.float32)
+                CO[k, K_C] = jnp.zeros(VREG, jnp.float32)
             else:
-                CO[k, 1] = CO[k - 1, 3]
-            CO[k, 2] = inv
-            CO[k, 3] = b_new
+                CO[k, K_C] = CO[k - 1, K_B]
+            CO[k, K_INV] = inv
+            CO[k, K_B] = b_new
 
     set_coefs(0, a_first, b_first)
 
     def gram_start(total):
-        rho = full_sum(jnp.where((row == 0) & (lane == 0), total, 0.0))
-        one = jnp.where(lane == 0, 1.0, 0.0)
+        rho = full_sum(jnp.where((row == 0) & (lane == 0), total, NIL))
+        one = jnp.where(lane == 0, 1.0, NIL)
         ST[S_G] = one * rho
         ST[S_CL] = one
         ST[S_DL] = one
@@ -426,13 +458,13 @@
         g, gp, cl, dl = ST[S_G], ST[S_GP], ST[S_CL], ST[S_DL]
         e_row, d_row = ST[S_E], ST[S_D]
         rho, lead = ST[S_RHO], ST[S_LEAD]
-        b_k, c_k, a_k = CO[k, 3], CO[k, 1], CO[k, 0]
+        b_k, c_k, a_k = CO[k, K_B], CO[k, K_C], CO[k, K_A]
         at_k, at_k1 = lane == k, lane == k + 1
-        rec = ((a - a_k) * g + b * turn(g, 127)
-               + c * turn(g, 1) - c_k * gp) * CO[k, 2]
-        g_new = jnp.where(lane < k, rec, jnp.where(at_k, e_row, jnp.where(at_k1, d_row, 0.0)))
+        rec = ((a - a_k) * g + b * turn(g, LAST)
+               + c * turn(g, 1) - c_k * gp) * CO[k, K_INV]
+        g_new = jnp.where(lane < k, rec, jnp.where(at_k, e_row, jnp.where(at_k1, d_row, NIL)))
         g_full = jnp.where(at_k1, turn(e_row, 1), g)
-        image = a * dl + turn(b * dl, 1) + turn(c * dl, 127)
+        image = a * dl + turn(b * dl, 1) + turn(c * dl, LAST)
         delta = lead * lane_sum(image * g_full)
         alpha = rho / delta
         y = ST[S_Y] + alpha * dl
@@ -440,7 +472,7 @@
         lead = -alpha * b_k * lead
         prod = cl * g_new
         rho_new = lead * lane_sum(prod)
-        size = jnp.abs(lead) * lane_sum(jnp.abs(prod))
+        size = lane_sum(jnp.abs(cl) * jnp.where(lane < k + 2, jnp.sqrt(jnp.maximum(d_row, NIL)), NIL))
         beta = rho_new / rho
         dl = cl + beta * dl
         ST[S_G], ST[S_GP], ST[S_CL], ST[S_DL] = g_new, g, cl, dl
@@ -451,8 +483,8 @@
         ST[S_LA] = inv_alpha + ST[S_BA]
         ST[S_LB] = jnp.sqrt(jnp.abs(beta)) * inv_alpha
         ST[S_BA] = beta * inv_alpha
-        err = size / jnp.abs(rho_new) * jnp.sqrt(jnp.abs(rho_new) / ST[S_RHO0])
-        err = jnp.where(rho_new > 0.0, err, 1e30)
+        err = size * size / jnp.sqrt(jnp.abs(rho_new) * ST[S_RHO0])
+        err = jnp.where(rho_new > NIL, err, 1e30)
         ST[S_ERR] = jnp.maximum(ST[S_ERR], jnp.where(err < 1e30, err, 1e30))
 
     def renew(k0):
@@ -463,19 +495,27 @@
         b_new = jnp.where(a_ok & (b_new > 0.25 * b_first) & (b_new < 2.0 * b_first), b_new, b_first)
         set_coefs(k0, a_new, b_new)
 
+    def prepare(k):
+        before = jnp.maximum(k - 1, 0)
+        cols = (PKS[k + 1, 0], PKS[k + 1, 1])
+        own = own_faces(cols)
+        for h, u in enumerate(cols):
+            PRE[h] = (CB[C_D, h] - CO[k, K_A]) * u - own[h] - CO[k, K_C] * PKS[before + 1, h]
+
     def apply_step(k):
         take_halo(k)
         for h in TILES:
             HK[h] = H[k + 1, h] * KYH[h]
         before = jnp.maximum(k - 1, 0)
-        cols = with_ghosts(PKS[k + 1, 0], PKS[k + 1, 1], Z[k, tb, pl.ds(0, NZ), :], Z[k, tb, pl.ds(HI, NZ), :])
+        far = outer_faces(Z[k, tb, pl.ds(0, NZ), :], Z[k, tb, pl.ds(HI, NZ), :], (H[k + 1, 0], H[k + 1, 1]))
         for h in TILES:
-            u = cols[h]
-            val = (CB[0, h] - CO[k, 0]) * u - CB[3, h] * own_layout(H[k + 1, h]) - CB[4, h] * UI[h]
-            val = val - CB[1, h] * turn(u, 125) - CB[2, h] * turn(u, 3)
-            val = val - CB[5, h] * z_up(u) - CB[6, h] * z_down(u) - CO[k, 1] * PKS[before + 1, h]
-            PKS[k + 2, h] = val * CO[k, 2]
-        a_k, c_k, i_k = three(CO[k, 0]), three(CO[k, 1]), three(CO[k, 2])
+            PKS[k + 2, h] = (PRE[h] - far[h]) * CO[k, K_INV]
+
+        @pl.when(k < ITERS - 1)
+        def _():
+            y_copy(k + 1).start()
+
+        a_k, c_k, i_k = three(CO[k, K_A]), three(CO[k, K_C]), three(CO[k, K_INV])
 
         def plane(i, carry, state):
             dots, cross = carry
@@ -492,12 +532,9 @@
             return (dots, cross), state
 
         vec = lambda t, q: Z[k, t, pl.ds(q, NZ), :]
-        more = k < ITERS - 1
-        dots, cross = sweep(vec, plane, k + 1, (zero24, zero24), more, lambda: y_copy(k + 1).start())
-
-        @pl.when(more)
-        def _():
-            pack(Z.at[k + 1], NZ, inner, UI)
+        dots, cross = sweep(vec, plane, k + 1, (zero24, zero24), k < ITERS - 1)
+
+        pack(Z.at[k + 1], NZ, inner, UI)
 
         tile = jnp.where((row == 0) & (lane == k + 1), full_sum(dots), PT[...])
         tile = jnp.where((row == 1) & (lane == k), full_sum(cross), tile)
@@ -523,6 +560,9 @@
             @pl.when(k == at)
             def _():
                 renew(k0)
+        prepare(jnp.minimum(k + 1, ITERS - 1))
+
+    prepare(0)
 
     @pl.loop(0, ITERS)
     def _(k):
@@ -536,24 +576,24 @@
 
     y = ST[S_Y]
     for k in range(ITERS):
-        YB[k] = lane_sum(jnp.where(lane == k, y, 0.0))
+        YB[k] = lane_sum(jnp.where(lane == k, y, NIL))
     hist = jnp.sqrt(ST[S_HIST] * (1.0 / cells))
     hist_ref[...] = jnp.where(row == 0, hist, ST[S_ERR])
 
     def combine(i, c):
-        r = rowsof(i + 1)
-        acc = [X0[t, pl.ds(r, NZ), :] for t in TILES]
+        r = rowsof(2 * i + 1)
+        acc = [X0[t, pl.ds(r, 2 * NZ), :] for t in TILES]
         for k in range(ITERS):
-            w = three(YB[k])
+            w = jnp.concatenate([YB[k]] * 6, axis=0)
             for t in TILES:
-                acc[t] = acc[t] + w * Z[k, t, pl.ds(r, NZ), :]
-        for t in TILES:
-            X0[t, pl.ds(r, NZ), :] = acc[t]
+                acc[t] = acc[t] + w * Z[k, t, pl.ds(r, 2 * NZ), :]
+        for t in TILES:
+            X0[t, pl.ds(r, 2 * NZ), :] = acc[t]
         return c
 
     outs = []
     for part in range(4):
-        lax.fori_loop(16 * part, 16 * part + 16, combine, 0)
+        lax.fori_loop(8 * part, 8 * part + 8, combine, 0)
         for t in TILES:
             cp = pltpu.make_async_copy(X0.at[t, pl.ds(NZ + 16 * NZ * part, 16 * NZ), :],
                                        out_h.at[pl.ds(16 * NZ * part, 16 * NZ), pl.ds(LANES * t, LANES)],
@@ -613,16 +653,17 @@
             pltpu.VMEM((ITERS + 1, 2, FULL, LANES), f32),
             pltpu.VMEM((2, FULL, LANES), f32),
             pltpu.VMEM((2, BODY, LANES), f32),
-            pltpu.VMEM((2, BODY + NZ, LANES), f32),
+            pltpu.VMEM((2, BODY + 32, LANES), f32),
             pltpu.VMEM((2, BODY, LANES), f32),
-            pltpu.VMEM((2, BODY + 8, LANES), f32),
+            pltpu.VMEM((2, BODY + 16, LANES), f32),
             pltpu.VMEM((ITERS + 2, 2, *VREG), f32),
             pltpu.VMEM((ITERS + 2, 2, *VREG), f32),
             pltpu.VMEM((2, *VREG), f32),
             pltpu.VMEM((2, *VREG), f32),
             pltpu.VMEM((2, *VREG), f32),
             pltpu.VMEM((2, *VREG), f32),
-            pltpu.VMEM((7, 2, *VREG), f32),
+            pltpu.VMEM((TOP, 2, *VREG), f32),
+            pltpu.VMEM((2, *VREG), f32),
             pltpu.VMEM((5, *VREG), f32),
             pltpu.VMEM((5, 8, *VREG), f32),
             pltpu.VMEM(VREG, f32),
@@ -633,24 +674,84 @@
             pltpu.SemaphoreType.DMA((8,)),
             pltpu.SemaphoreType.DMA((8,)),
             pltpu.SemaphoreType.DMA((8,)),
-            pltpu.SemaphoreType.DMA((ITERS, 3)),
-            pltpu.SemaphoreType.DMA((ITERS, 3)),
-            pltpu.SemaphoreType.DMA((5, 7)),
+            pltpu.SemaphoreType.DMA((ITERS, NQ)),
+            pltpu.SemaphoreType.DMA((ITERS, NQ)),
+            pltpu.SemaphoreType.DMA((5, TOP)),
             pltpu.SemaphoreType.DMA((5,)),
         ],
         compiler_params=pltpu.CompilerParams(collective_id=0, has_side_effects=True,
-                                             vmem_limit_bytes=60 * 1024 * 1024),
+                                             vmem_limit_bytes=65011712),
     )(*(flat(v) for v in (shift, rhs_field, x_init, cond_x, cond_y, cond_z)))
     x_out = jnp.transpose(x_rows.reshape(NX, NZ, 256), (0, 2, 1))
     return x_out, small[0, :ITERS + 1], small[1, 0]
 
 
+def classic_solve(shift, rhs_field, x_init, cond_x, cond_y, cond_z):
+    count_x, count_y = 4, 2
+    fwd_x = [(src, src + 1) for src in range(count_x - 1)]
+    back_x = [(src + 1, src) for src in range(count_x - 1)]
+    pos_x, pos_y = lax.axis_index("px"), lax.axis_index("py")
+    plane_x = lax.broadcasted_iota(jnp.int32, (NX, 1, 1), 0)
+    plane_y = lax.broadcasted_iota(jnp.int32, (1, ROW, 1), 1)
+    plane_z = lax.broadcasted_iota(jnp.int32, (1, 1, NZ), 2)
+    plus_x = jnp.where((pos_x == count_x - 1) & (plane_x == NX - 1), NIL, cond_x)
+    plus_y = jnp.where((pos_y == count_y - 1) & (plane_y == ROW - 1), NIL, cond_y)
+    plus_z = jnp.where(plane_z == NZ - 1, NIL, cond_z)
+
+    def shifted(vec, axis, ahead, halo):
+        size = vec.shape[axis]
+        if ahead:
+            return jnp.concatenate([lax.slice_in_dim(vec, 1, size, axis=axis), halo], axis=axis)
+        return jnp.concatenate([halo, lax.slice_in_dim(vec, 0, size - 1, axis=axis)], axis=axis)
+
+    def below(vec):
+        low_x = lax.ppermute(vec[-1:], "px", fwd_x)
+        low_y = lax.ppermute(vec[:, -1:], "py", [(0, 1)])
+        return (shifted(vec, 0, False, low_x), shifted(vec, 1, False, low_y),
+                shifted(vec, 2, False, jnp.zeros_like(vec[:, :, :1])))
+
+    def above(vec):
+        high_x = lax.ppermute(vec[:1], "px", back_x)
+        high_y = lax.ppermute(vec[:, :1], "py", [(1, 0)])
+        return (shifted(vec, 0, True, high_x), shifted(vec, 1, True, high_y),
+                shifted(vec, 2, True, jnp.zeros_like(vec[:, :, :1])))
+
+    minus_x, minus_y, minus_z = below(plus_x)[0], below(plus_y)[1], below(plus_z)[2]
+    diag = shift + plus_x + minus_x + plus_y + minus_y + plus_z + minus_z
+
+    def apply_op(vec):
+        up_x, up_y, up_z = above(vec)
+        down_x, down_y, down_z = below(vec)
+        return (diag * vec - plus_x * up_x - minus_x * down_x
+                - plus_y * up_y - minus_y * down_y - plus_z * up_z - minus_z * down_z)
+
+    def global_dot(left, right):
+        return lax.psum(jnp.sum(left * right), SUM_AXES)
+
+    res = rhs_field - apply_op(x_init)
+    rho = global_dot(res, res)
+    history = jnp.where(jnp.arange(ITERS + 1) == 0, rho, NIL)
+
+    def step(k, state):
+        x, res, p, rho, history = state
+        q = apply_op(p)
+        alpha = rho / global_dot(p, q)
+        x = x + alpha * p
+        res = res - alpha * q
+        rho_new = global_dot(res, res)
+        p = res + (rho_new / rho) * p
+        return x, res, p, rho_new, jnp.where(jnp.arange(ITERS + 1) == k + 1, rho_new, history)
+
+    x, _, _, _, history = lax.fori_loop(0, ITERS, step, (jnp.zeros_like(res), res, res, rho, history))
+    return x_init + x, jnp.sqrt(history / CELLS)
+
+
 def solution(mesh):
     field_spec = P("px", "py", None)
 
     def local_solve(*fields):
-        x_out, history, _ = fused_solve(*fields)
-        return x_out, history
+        x_out, history, err = fused_solve(*fields)
+        return lax.cond(err < ERR_LIMIT, lambda: (x_out, history), lambda: classic_solve(*fields))
 
     return jax.shard_map(local_solve, mesh=mesh, in_specs=(field_spec,) * 6,
                          out_specs=(field_spec, P()), check_vma=False)

time: 92 us -> 82.8 us (0.900)
  Pallas kernels: 87.3 us -> 77.9 us
    pallas_call x1, Pallas kernels: 87.3 us -> 77.9 us  [fused_solve(): pl.pallas_call(kernel, out_shape=(jax.ShapeDtypeStruct((BODY, 256), f32),...]
    squeeze x1, local copies, waits for them, and re-layouts: 1.2 us -> 0.01 us  [fused_solve(): return (x_out, small[0, :ITERS + 1], small[1, 0])]
    unnamed x1 -> x5, local copies, waits for them, and re-layouts: 2.65 us -> 2.66 us
where the time goes in v4:
time: 82.8 us; the launch traced here: 82.6 us
  Pallas kernels  77.9 us (94%)
  local copies, waits for them, and re-layouts  3.18 us (4%)
  between operations  1.32 us (2%)
    pallas_call x1, Pallas kernels, fused_solve(): pl.pallas_call(kernel, out_shape=(jax.ShapeDtypeStruct((BODY, 256), f32),...  77.9 us
    unnamed x5, local copies, waits for them, and re-layouts  2.66 us

profile of v4, /device:TPU:0, one launch (start us, length us, event | category | flops | bytes accessed | tf_op | source)
XLA Modules:
  0.0 82.6 jit_solution(10475164473729626598)
XLA Ops:
  0.6 0.0 copy-start
  0.6 77.9 %shard_map.81 = (f32[1536,256]{1,0:T(8,128)}, f32[8,128]{1,0:T(8,128)S(1)}) custom-call(f32[1536,256]{1,0:T(8,128)} %bitcast.33, f32[1536,256]{1,0:T(8,128)} %bitcast.34, f32[1536,256]{1,0:T(8,128)} %bitcast.26, f32[1536,256]{1,0:T(8,128)} %bitcast.30, f32[1536,256]{1,0:T(8,128)} %bitcast.31, f32[1536,256]{1,0:T(8,128)} %bitcast.32), custom_call_target="tpu_custom_call" | custom-call | tf_op jit(solution)/shard_map/pallas_call | solution.py:647
  78.5 0.5 slice.122
  79.7 0.0 copy-done
  79.7 0.2 conditional.1
  80.0 0.0 copy-start.17
  80.0 2.7 %copy.69 = f32[64,256,24]{1,2,0:T(8,128)} copy(f32[64,256,24]{1,2,0:T(8,128)} %get-tuple-element.521) | data formatting | bytes 3145728
  82.6 0.0 copy-done.17
  (1 shorter events, 0.0 us)
Async XLA Ops:
  0.6 79.1 %copy-start = (f32[64,256,24]{1,2,0:T(8,128)S(1)}, f32[64,256,24]{1,2,0:T(8,128)}, u32[]{:S(2)}) copy-start(f32[64,256,24]{1,2,0:T(8,128)} %param.12) | copy-start | bytes 4718596
  80.0 2.7 %copy-start.17 = (f32[21]{0:T(128)}, f32[21]{0:T(128)S(1)}, u32[]{:S(2)}) copy-start(f32[21]{0:T(128)S(1)} %get-tuple-element.522) | copy-start | bytes 256

commit v5 on v4

--- a/solution.py
+++ b/solution.py
@@ -19,11 +19,7 @@
 FULL = BODY + 2 * NZ
 HI = BODY + NZ
 OTHERS = tuple((dy, dx) for dy in range(2) for dx in range(4) if (dy, dx) != (0, 0))
-SEND_AT = {1: 4, 2: 9, 3: 15, 4: 19}
-TAKE_AT = {6: 1, 11: 2, 17: 3}
-STEPS_AT = {6: (0, 2), 7: (2, 4), 8: (4, 5), 11: (5, 7), 12: (7, 9), 13: (9, 10),
-            17: (10, 12), 18: (12, 14), 19: (14, 16)}
-RENEW_AT = {8: 9, 13: 14}
+RENEW_AT = (7, 12)
 VREG = (8, 128)
 SUB, LANES = VREG
 TILES = range(2)
@@ -43,7 +39,7 @@
     return pltpu.roll(v, by, 0)
 
 
-S_A, S_B, S_C, S_GP, S_G, S_CL, S_DL, S_Y, S_RHO, S_LEAD, S_HIST, S_BA, S_LA, S_LB, S_LA2, S_LB2, S_ERR, S_D, S_E, S_RHO0 = range(20)
+S_A, S_B, S_C, S_GP, S_G, S_CL, S_DL, S_Y, S_RHO, S_LEAD, S_HIST, S_BA, S_LA, S_LB, S_LA2, S_LB2, S_ERR, S_D, S_AL, S_RHO0 = range(20)
 
 
 def lanes():
@@ -67,7 +63,7 @@
 
 
 def kernel(s_h, b_h, x0_h, kx_h, ky_h, kz_h, out_h, hist_ref,
-           Z, X0, D, KX, KY, KZ, PKS, H, KYP, KYH, HK, UI, CB, PRE, RS, RR, PT, ST, CO, YB,
+           Z, X0, D, KX, KY, KZ, PKS, H, KYP, KYH, HK, UI, CB, PRE, XS, XG, RS, RR, PT, ST, CO, YB,
            lsem, osem, is_s, is_r, hs, hr, rs, rr):
     px, py = lax.axis_index("px"), lax.axis_index("py")
     me = py * 4 + px
@@ -79,12 +75,13 @@
 
     loads = []
     for n, (src, dst, base) in enumerate((
-            (ky_h, KY, 0), (x0_h, X0, NZ), (kx_h, KX, NZ), (kz_h, KZ, 8), (s_h, D, 0), (b_h, None, NZ))):
+            (ky_h, KY, 0), (x0_h, X0, NZ), (kx_h, KX, NZ), (s_h, D, 0), (b_h, None, NZ), (kz_h, KZ, 8))):
         for t in TILES:
             to = Z.at[0, t, pl.ds(base, BODY), :] if dst is None else dst.at[t, pl.ds(base, BODY), :]
             cp = pltpu.make_async_copy(src.at[:, pl.ds(LANES * t, LANES)], to, lsem.at[2 * n + t])
-            cp.start()
             loads.append(cp)
+    for cp in loads[:4]:
+        cp.start()
 
     zero_plane = jnp.zeros((NZ, LANES), jnp.float32)
     for t in TILES:
@@ -93,6 +90,9 @@
         X0[t, pl.ds(HI, NZ), :] = zero_plane
         KZ[t, pl.ds(0, 8), :] = jnp.zeros(VREG, jnp.float32)
     KYH[...] = jnp.zeros((2, *VREG), jnp.float32)
+    for t in TILES:
+        for k in range(ITERS + 2):
+            XG[k, t] = jnp.zeros(VREG, jnp.float32)
 
     @pl.loop(0, ITERS + 1)
     def _(k):
@@ -136,7 +136,6 @@
             for cp in init_down(t):
                 cp.start()
 
-    off = 1 - py
     tb = 1 - py
     edge = LAST * (1 - py)
     inner = 126 + py * (1 - 126)
@@ -153,27 +152,25 @@
         return out
 
     def pack(ref, base, bl, dst):
-        start = NQ + off - bl + LANES
+        start = NQ - bl + LANES
         for h in TILES:
             accs = [jnp.zeros(VREG, jnp.float32)] * NQ
             for a in range(NQ * HALF):
                 v = ref[tb, pl.ds(base + HALF * NZ * h + SUB * a, SUB), :]
                 moved = turn(v, lax.rem(start + a, LANES))
-                accs[a % NQ] = jnp.where(lane == a + NQ + off, moved, accs[a % NQ])
+                accs[a % NQ] = jnp.where(lane == a + NQ, moved, accs[a % NQ])
             dst[h] = accs[0] + accs[1] + accs[2]
 
-    low_ghost = (lane >= off) & (lane < off + NQ)
-    high_ghost = (lane >= off + 99) & (lane < off + 102)
+    from_lo, from_hi = (lane >= NQ) & (lane < 6), (lane >= NQ * HALF) & (lane < NQ * HALF + NQ)
+    low_ghost = lane < NQ
+    high_ghost = (lane >= 99) & (lane < 102)
 
     def with_ghosts(n0, n1, lo, hi):
-        lo = turn(pack_one([lo[SUB * q:SUB * q + SUB] for q in range(NQ)], edge), lax.rem(off - edge + LANES, LANES))
-        hi = turn(pack_one([hi[SUB * q:SUB * q + SUB] for q in range(NQ)], edge), lax.rem(99 + off - edge + LANES, LANES))
+        lo = turn(pack_one([lo[SUB * q:SUB * q + SUB] for q in range(NQ)], edge), lax.rem(LANES - edge, LANES))
+        hi = turn(pack_one([hi[SUB * q:SUB * q + SUB] for q in range(NQ)], edge), lax.rem(99 - edge + LANES, LANES))
         return (jnp.where(low_ghost, lo, jnp.where(high_ghost, turn(n1, 96), n0)),
                 jnp.where(low_ghost, turn(n0, 32), jnp.where(high_ghost, hi, n1)))
 
-    def own_layout(v):
-        return turn(v, 1 + py * 126)
-
     def z_up(v):
         return jnp.where(row == TOP, lift(turn(v, LAST), TOP), lift(v, TOP))
 
@@ -181,14 +178,16 @@
         return jnp.where(row == 0, lift(turn(v, 1), 1), lift(v, 1))
 
     def unpack(tile, j):
-        parts = [turn(tile, 124 - (NQ * j + q)) for q in range(NQ)]
+        parts = [turn(tile, 124 + py - (NQ * j + q)) for q in range(NQ)]
         return jnp.concatenate(parts, axis=0)
 
     def rowsof(i):
         return pl.multiple_of(NZ * i, 8)
 
-    loads[0].wait()
-    loads[1].wait()
+    for cp in loads[:4]:
+        cp.wait()
+    for cp in loads[4:]:
+        cp.start()
     pack(KY, 0, edge, KYP)
     ky_copy = remote(KYP, KYH, is_s.at[6], is_r.at[6], to_y)
 
@@ -196,13 +195,22 @@
     def _():
         ky_copy.start()
 
-    loads[2].wait()
-    loads[NQ].wait()
     pack(X0, NZ, edge, PKS.at[0])
     x0_copy = remote(PKS.at[0], H.at[0], is_s.at[TOP], is_r.at[TOP], to_y)
     x0_copy.start()
 
-    for cp in loads[4:12]:
+    pack(X0, NZ, inner, UI)
+    pack(KY, 0, inner, CB.at[C_IN])
+    for cp in loads[4:6]:
+        cp.wait()
+    pack(KX, NZ, edge, CB.at[C_UP])
+    for cp in loads[6:8]:
+        cp.wait()
+    pack(D, 0, edge, CB.at[C_D])
+    for cp in loads[8:10]:
+        cp.wait()
+    pack(Z.at[0], NZ, edge, PRE)
+    for cp in loads[10:]:
         cp.wait()
 
     keep_x = jnp.where(has_hi, 1.0, NIL)
@@ -243,21 +251,26 @@
         for cp in sum_copies(e):
             cp.start()
 
-    def sum_take(e):
+    def sum_wait(e):
         pltpu.make_async_copy(RR.at[e, pl.ds(0, TOP)], RR.at[e, pl.ds(0, TOP)], rr.at[e]).wait()
+
+    def sum_total(e):
         total = RR[e, 0]
         for n in range(1, 8):
             total = total + RR[e, n]
         return total
 
+    def sum_take(e):
+        sum_wait(e)
+        return sum_total(e)
+
     sum_send(0, stats)
-    pack(D, 0, edge, CB.at[C_D])
-    pack(Z.at[0], NZ, edge, PRE)
-    pack(X0, NZ, inner, UI)
-    pack(KX, NZ, edge, CB.at[C_UP])
+    for h in TILES:
+        last_x = (lane >= NQ * HALF) & (lane < NQ * HALF + NQ)
+        if h == 1:
+            CB[C_UP, h] = jnp.where(last_x, CB[C_UP, h] * keep_x, CB[C_UP, h])
+        CB[C_OUT, h] = KYP[h]
     pack(KZ, 8, edge, CB.at[C_ZUP])
-    pack(KY, 0, inner, CB.at[C_IN])
-    pack(KY, 0, edge, CB.at[C_OUT])
     for h in TILES:
         CB[C_ZDN, h] = z_down(CB[C_ZUP, h])
 
@@ -270,6 +283,36 @@
     def y_copy(k):
         return remote(PKS.at[k + 1], H.at[k + 1], hs.at[k, 2], hr.at[k, 2], to_y)
 
+    def edge_up(k):
+        return remote(XS.at[k + 1, 0], XG.at[k + 1, 0], hs.at[k, NQ], hr.at[k, NQ], to_x(1))
+
+    def edge_down(k):
+        return remote(XS.at[k + 1, 1], XG.at[k + 1, 1], hs.at[k, 4], hr.at[k, 4], to_x(-1))
+
+    def send_column(k):
+        y_copy(k).start()
+        XS[k + 1, 0] = jnp.where(from_lo, turn(PKS[k + 1, 1], 35), NIL)
+        XS[k + 1, 1] = jnp.where(from_hi, turn(PKS[k + 1, 0], 93), NIL)
+
+        @pl.when(has_hi)
+        def _():
+            edge_up(k).start()
+
+        @pl.when(has_lo)
+        def _():
+            edge_down(k).start()
+
+    def take_column(k):
+        @pl.when(has_lo)
+        def _():
+            edge_up(k).wait_recv()
+
+        @pl.when(has_hi)
+        def _():
+            edge_down(k).wait_recv()
+
+        y_copy(k).wait_recv()
+
     def send_x(k):
         @pl.when(has_hi)
         def _():
@@ -288,7 +331,6 @@
         def _():
             down_copy(k).wait_recv()
 
-        y_copy(k).wait_recv()
 
     def first_state(vec, i):
         r = rowsof(i)
@@ -337,7 +379,6 @@
 
     def own_faces(cols):
         n0, n1 = cols
-        from_lo, from_hi = (lane >= off + NQ) & (lane < off + 6), (lane >= off + NQ * HALF) & (lane < off + NQ * HALF + NQ)
         down = (jnp.where(from_lo, NIL, turn(n0, NQ)), jnp.where(from_lo, turn(n0, 35), turn(n1, NQ)))
         up = (jnp.where(from_hi, turn(n1, 93), turn(n0, 125)), jnp.where(from_hi, NIL, turn(n1, 125)))
         return [CB[C_IN, h] * UI[h] + CB[C_UP, h] * up[h] + CB[C_DOWN, h] * down[h]
@@ -347,10 +388,10 @@
         ghost = [jnp.zeros(VREG, jnp.float32)] * 2
         for q in range(NQ):
             for h, (v, at) in enumerate(((lo, NQ), (hi, NQ * HALF))):
-                at = at + q + off
+                at = at + q
                 moved = turn(v[SUB * q:SUB * q + SUB], lax.rem(at - edge + LANES, LANES))
                 ghost[h] = jnp.where(lane == at, moved, ghost[h])
-        return [CB[C_OUT, h] * own_layout(beyond[h]) + CB[C_DOWN - h, h] * ghost[h] for h in TILES]
+        return [CB[C_OUT, h] * beyond[h] + CB[C_DOWN - h, h] * ghost[h] for h in TILES]
 
     x0_vec = lambda t, q: X0[t, pl.ds(q, NZ), :]
 
@@ -371,7 +412,7 @@
             rho = rho + res * res
         return rho, state
 
-    UNROLL = 10
+    UNROLL = 31
 
     def sweep(vec, plane, k, sums1, more):
         def run(i, n, c):
@@ -386,8 +427,7 @@
         def _():
             send_x(k)
 
-        sums1 = run(NX - 2, 1, run(1, 1, sums1))
-        return lax.fori_loop(0, 60 // UNROLL, lambda m, c: run(2 + UNROLL * m, UNROLL, c), sums1)
+        return lax.fori_loop(0, (NX - 2) // UNROLL, lambda m, c: run(1 + UNROLL * m, UNROLL, c), sums1)
 
     zero24 = zero_plane
     zero_tile = zero_plane
@@ -395,7 +435,7 @@
     for h in TILES:
         CB[C_DOWN, h] = turn(kx_cols[h], NQ)
         ky_edge, ky_in = CB[C_OUT, h], CB[C_IN, h]
-        CB[C_OUT, h] = jnp.where(py == 0, ky_edge, own_layout(KYH[h]))
+        CB[C_OUT, h] = jnp.where(py == 0, ky_edge, KYH[h])
         CB[C_IN, h] = jnp.where(py == 0, ky_in, ky_edge)
     far = outer_faces(X0[tb, pl.ds(0, NZ), :], X0[tb, pl.ds(HI, NZ), :], (H[0, 0], H[0, 1]))
     own = own_faces((PKS[0, 0], PKS[0, 1]))
@@ -403,7 +443,7 @@
         diag = CB[C_D, h] + CB[C_UP, h] + CB[C_DOWN, h] + CB[C_OUT, h] + CB[C_IN, h] + CB[C_ZUP, h] + CB[C_ZDN, h]
         CB[C_D, h] = diag
         PKS[1, h] = PRE[h] - (diag * PKS[0, h] - far[h] - own[h])
-    y_copy(0).start()
+    send_column(0)
     rho0 = sweep(x0_vec, start_plane, 0, zero24, px >= 0)
     pack(Z.at[0], NZ, inner, UI)
     PT[...] = jnp.where((row == 0) & (lane == 0), full_sum(rho0), NIL)
@@ -441,6 +481,8 @@
     def gram_start(total):
         rho = full_sum(jnp.where((row == 0) & (lane == 0), total, NIL))
         one = jnp.where(lane == 0, 1.0, NIL)
+        for n in (S_GP, S_Y, S_BA, S_LA, S_LB, S_LA2, S_LB2, S_ERR):
+            ST[n] = jnp.zeros(VREG, jnp.float32)
         ST[S_G] = one * rho
         ST[S_CL] = one
         ST[S_DL] = one
@@ -449,14 +491,10 @@
         ST[S_RHO0] = rho
         ST[S_HIST] = one * rho
 
-    def gram_load(total):
-        ST[S_D] = jnp.broadcast_to(total[0:1], VREG)
-        ST[S_E] = jnp.broadcast_to(total[1:2], VREG)
-
-    def gram_step(k):
+    def gram_step(k, total):
         a, b, c = ST[S_A], ST[S_B], ST[S_C]
         g, gp, cl, dl = ST[S_G], ST[S_GP], ST[S_CL], ST[S_DL]
-        e_row, d_row = ST[S_E], ST[S_D]
+        d_row, e_row = jnp.broadcast_to(total[0:1], VREG), jnp.broadcast_to(total[1:2], VREG)
         rho, lead = ST[S_RHO], ST[S_LEAD]
         b_k, c_k, a_k = CO[k, K_B], CO[k, K_C], CO[k, K_A]
         at_k, at_k1 = lane == k, lane == k + 1
@@ -467,6 +505,7 @@
         image = a * dl + turn(b * dl, 1) + turn(c * dl, LAST)
         delta = lead * lane_sum(image * g_full)
         alpha = rho / delta
+        ST[S_AL] = alpha
         y = ST[S_Y] + alpha * dl
         cl = cl - alpha * image
         lead = -alpha * b_k * lead
@@ -503,18 +542,19 @@
             PRE[h] = (CB[C_D, h] - CO[k, K_A]) * u - own[h] - CO[k, K_C] * PKS[before + 1, h]
 
     def apply_step(k):
-        take_halo(k)
+        take_column(k)
+        before = jnp.maximum(k - 1, 0)
+        for h in TILES:
+            far = CB[C_OUT, h] * H[k + 1, h] + CB[C_DOWN - h, h] * XG[k + 1, h]
+            PKS[k + 2, h] = (PRE[h] - far) * CO[k, K_INV]
+
+        @pl.when(k < ITERS - 1)
+        def _():
+            send_column(k + 1)
+
         for h in TILES:
             HK[h] = H[k + 1, h] * KYH[h]
-        before = jnp.maximum(k - 1, 0)
-        far = outer_faces(Z[k, tb, pl.ds(0, NZ), :], Z[k, tb, pl.ds(HI, NZ), :], (H[k + 1, 0], H[k + 1, 1]))
-        for h in TILES:
-            PKS[k + 2, h] = (PRE[h] - far[h]) * CO[k, K_INV]
-
-        @pl.when(k < ITERS - 1)
-        def _():
-            y_copy(k + 1).start()
-
+        take_halo(k)
         a_k, c_k, i_k = three(CO[k, K_A]), three(CO[k, K_C]), three(CO[k, K_INV])
 
         def plane(i, carry, state):
@@ -534,33 +574,29 @@
         vec = lambda t, q: Z[k, t, pl.ds(q, NZ), :]
         dots, cross = sweep(vec, plane, k + 1, (zero24, zero24), k < ITERS - 1)
 
+        step = k - 2
+
+        @pl.when(step > 0)
+        def _():
+            sum_wait(step + 1)
+
+        total = sum_total(jnp.maximum(step + 1, 0))
         pack(Z.at[k + 1], NZ, inner, UI)
-
         tile = jnp.where((row == 0) & (lane == k + 1), full_sum(dots), PT[...])
         tile = jnp.where((row == 1) & (lane == k), full_sum(cross), tile)
         PT[...] = tile
-        for e, at in SEND_AT.items():
+        gram_step(jnp.maximum(step, 0), total)
+        prepare(jnp.minimum(k + 1, ITERS - 1))
+        sum_send(k + 1, tile)
+
+        @pl.when(k == 1)
+        def _():
+            gram_start(sum_take(1))
+
+        for at in RENEW_AT:
             @pl.when(k == at)
             def _():
-                sum_send(e, tile)
-        for at, e in TAKE_AT.items():
-            @pl.when(k == at)
-            def _():
-                total = sum_take(e)
-                gram_load(total)
-                if e == 1:
-                    gram_start(total)
-        for at, (lo, hi) in STEPS_AT.items():
-            @pl.when(k == at)
-            def _():
-                @pl.loop(lo, hi)
-                def _(s):
-                    gram_step(s)
-        for at, k0 in RENEW_AT.items():
-            @pl.when(k == at)
-            def _():
-                renew(k0)
-        prepare(jnp.minimum(k + 1, ITERS - 1))
+                renew(at + 2)
 
     prepare(0)
 
@@ -568,32 +604,63 @@
     def _(k):
         apply_step(k)
 
-    gram_load(sum_take(4))
-
-    @pl.loop(16, ITERS)
-    def _(s):
-        gram_step(s)
-
+    gram_step(ITERS - 2, sum_take(ITERS - 1))
+
+    y, d = ST[S_Y], ST[S_DL]
+    for k in range(ITERS):
+        YB[k] = lane_sum(jnp.where(lane == k, y, NIL))
+        YB[ITERS + k] = lane_sum(jnp.where(lane == k, d, NIL))
+
+    AHEAD = 32
+
+    def combine(i, c):
+        r = rowsof(i + 1)
+        acc = [X0[t, pl.ds(r, NZ), :] for t in TILES]
+        way = [zero_plane, zero_plane]
+        for k in range(ITERS):
+            w, v = three(YB[k]), three(YB[ITERS + k])
+            for t in TILES:
+                z = Z[k, t, pl.ds(r, NZ), :]
+                way[t] = way[t] + v * z
+                if k < ITERS - 1:
+                    acc[t] = acc[t] + w * z
+        for t in TILES:
+            X0[t, pl.ds(r, NZ), :] = acc[t]
+            Z[ITERS, t, pl.ds(r, NZ), :] = way[t]
+        return c
+
+    lax.fori_loop(0, AHEAD, combine, 0, unroll=2)
+    gram_step(ITERS - 1, sum_take(ITERS))
     y = ST[S_Y]
     for k in range(ITERS):
         YB[k] = lane_sum(jnp.where(lane == k, y, NIL))
     hist = jnp.sqrt(ST[S_HIST] * (1.0 / cells))
     hist_ref[...] = jnp.where(row == 0, hist, ST[S_ERR])
-
-    def combine(i, c):
-        r = rowsof(2 * i + 1)
-        acc = [X0[t, pl.ds(r, 2 * NZ), :] for t in TILES]
+    alpha = three(ST[S_AL])
+
+    def last_step(i, c):
+        r = rowsof(i + 1)
+        for t in TILES:
+            X0[t, pl.ds(r, NZ), :] = X0[t, pl.ds(r, NZ), :] + alpha * Z[ITERS, t, pl.ds(r, NZ), :]
+        return c
+
+    def whole_step(i, c):
+        r = rowsof(i + 1)
+        acc = [X0[t, pl.ds(r, NZ), :] for t in TILES]
         for k in range(ITERS):
-            w = jnp.concatenate([YB[k]] * 6, axis=0)
+            w = three(YB[k])
             for t in TILES:
-                acc[t] = acc[t] + w * Z[k, t, pl.ds(r, 2 * NZ), :]
-        for t in TILES:
-            X0[t, pl.ds(r, 2 * NZ), :] = acc[t]
+                acc[t] = acc[t] + w * Z[k, t, pl.ds(r, NZ), :]
+        for t in TILES:
+            X0[t, pl.ds(r, NZ), :] = acc[t]
         return c
 
     outs = []
     for part in range(4):
-        lax.fori_loop(8 * part, 8 * part + 8, combine, 0)
+        if part < NQ:
+            lax.fori_loop(16 * part, min(16 * part + 16, AHEAD), last_step, 0, unroll=4)
+        if 16 * part + 16 > AHEAD:
+            lax.fori_loop(max(16 * part, AHEAD), 16 * part + 16, whole_step, 0, unroll=2)
         for t in TILES:
             cp = pltpu.make_async_copy(X0.at[t, pl.ds(NZ + 16 * NZ * part, 16 * NZ), :],
                                        out_h.at[pl.ds(16 * NZ * part, 16 * NZ), pl.ds(LANES * t, LANES)],
@@ -624,16 +691,20 @@
         @pl.when(has_hi)
         def _():
             up_copy(k).wait_send()
+            edge_up(k).wait_send()
 
         @pl.when(has_lo)
         def _():
             down_copy(k).wait_send()
+            edge_down(k).wait_send()
 
         y_copy(k).wait_send()
 
-    for e in range(5):
+    @pl.loop(0, ITERS + 1)
+    def _(e):
         for cp in sum_copies(e):
             cp.wait_send()
+
     for cp in outs:
         cp.wait()
 
@@ -664,20 +735,22 @@
             pltpu.VMEM((2, *VREG), f32),
             pltpu.VMEM((TOP, 2, *VREG), f32),
             pltpu.VMEM((2, *VREG), f32),
-            pltpu.VMEM((5, *VREG), f32),
-            pltpu.VMEM((5, 8, *VREG), f32),
+            pltpu.VMEM((ITERS + 2, 2, *VREG), f32),
+            pltpu.VMEM((ITERS + 2, 2, *VREG), f32),
+            pltpu.VMEM((ITERS + 1, *VREG), f32),
+            pltpu.VMEM((ITERS + 1, 8, *VREG), f32),
             pltpu.VMEM(VREG, f32),
             pltpu.VMEM((20, *VREG), f32),
             pltpu.VMEM((ITERS, 4, *VREG), f32),
-            pltpu.VMEM((ITERS, *VREG), f32),
+            pltpu.VMEM((2 * ITERS, *VREG), f32),
             pltpu.SemaphoreType.DMA((12,)),
             pltpu.SemaphoreType.DMA((8,)),
             pltpu.SemaphoreType.DMA((8,)),
             pltpu.SemaphoreType.DMA((8,)),
-            pltpu.SemaphoreType.DMA((ITERS, NQ)),
-            pltpu.SemaphoreType.DMA((ITERS, NQ)),
-            pltpu.SemaphoreType.DMA((5, TOP)),
-            pltpu.SemaphoreType.DMA((5,)),
+            pltpu.SemaphoreType.DMA((ITERS, 5)),
+            pltpu.SemaphoreType.DMA((ITERS, 5)),
+            pltpu.SemaphoreType.DMA((ITERS + 1, TOP)),
+            pltpu.SemaphoreType.DMA((ITERS + 1,)),
         ],
         compiler_params=pltpu.CompilerParams(collective_id=0, has_side_effects=True,
                                              vmem_limit_bytes=65011712),

time: 82.8 us -> 79.9 us (0.965)
  Pallas kernels: 77.9 us -> 75 us
    pallas_call x1, Pallas kernels: 77.9 us -> 75 us  [fused_solve(): pl.pallas_call(kernel, out_shape=(jax.ShapeDtypeStruct((BODY, 256), f32),...]
where the time goes in v5:
time: 79.9 us; the launch traced here: 79.8 us
  Pallas kernels  75 us (94%)
  local copies, waits for them, and re-layouts  3.18 us (4%)
  between operations  1.32 us (2%)
    pallas_call x1, Pallas kernels, fused_solve(): pl.pallas_call(kernel, out_shape=(jax.ShapeDtypeStruct((BODY, 256), f32),...  75 us
    unnamed x5, local copies, waits for them, and re-layouts  2.66 us

profile of v5, /device:TPU:0, one launch (start us, length us, event | category | flops | bytes accessed | tf_op | source)
XLA Modules:
  0.0 79.8 jit_solution(4679457584497954088)
XLA Ops:
  0.6 0.0 copy-start
  0.6 75.0 %shard_map.81 = (f32[1536,256]{1,0:T(8,128)}, f32[8,128]{1,0:T(8,128)S(1)}) custom-call(f32[1536,256]{1,0:T(8,128)} %bitcast.33, f32[1536,256]{1,0:T(8,128)} %bitcast.34, f32[1536,256]{1,0:T(8,128)} %bitcast.26, f32[1536,256]{1,0:T(8,128)} %bitcast.30, f32[1536,256]{1,0:T(8,128)} %bitcast.31, f32[1536,256]{1,0:T(8,128)} %bitcast.32), custom_call_target="tpu_custom_call" | custom-call | tf_op jit(solution)/shard_map/pallas_call | solution.py:718
  75.7 0.5 slice.122
  76.8 0.0 copy-done
  76.8 0.2 conditional.1
  77.1 0.0 copy-start.17
  77.1 2.7 %copy.69 = f32[64,256,24]{1,2,0:T(8,128)} copy(f32[64,256,24]{1,2,0:T(8,128)} %get-tuple-element.521) | data formatting | bytes 3145728
  79.7 0.0 copy-done.17
  (1 shorter events, 0.0 us)
Async XLA Ops:
  0.6 76.2 %copy-start = (f32[64,256,24]{1,2,0:T(8,128)S(1)}, f32[64,256,24]{1,2,0:T(8,128)}, u32[]{:S(2)}) copy-start(f32[64,256,24]{1,2,0:T(8,128)} %param.12) | copy-start | bytes 4718596
  77.1 2.7 %copy-start.17 = (f32[21]{0:T(128)}, f32[21]{0:T(128)S(1)}, u32[]{:S(2)}) copy-start(f32[21]{0:T(128)S(1)} %get-tuple-element.522) | copy-start | bytes 256

commit v6 on v5

--- a/solution.py
+++ b/solution.py
@@ -62,9 +62,9 @@
     return jnp.concatenate([v, v, v], axis=0)
 
 
-def kernel(s_h, b_h, x0_h, kx_h, ky_h, kz_h, out_h, hist_ref,
+def kernel(s_h, b_h, x0_h, kx_h, ky_h, kz_h, out_ref, hist_ref,
            Z, X0, D, KX, KY, KZ, PKS, H, KYP, KYH, HK, UI, CB, PRE, XS, XG, RS, RR, PT, ST, CO, YB,
-           lsem, osem, is_s, is_r, hs, hr, rs, rr):
+           lsem, is_s, is_r, hs, hr, rs, rr):
     px, py = lax.axis_index("px"), lax.axis_index("py")
     me = py * 4 + px
     lane, row = lanes(), rows8()
@@ -641,7 +641,7 @@
     def last_step(i, c):
         r = rowsof(i + 1)
         for t in TILES:
-            X0[t, pl.ds(r, NZ), :] = X0[t, pl.ds(r, NZ), :] + alpha * Z[ITERS, t, pl.ds(r, NZ), :]
+            out_ref[pl.ds(rowsof(i), NZ), LANES * t:LANES * t + LANES] = X0[t, pl.ds(r, NZ), :] + alpha * Z[ITERS, t, pl.ds(r, NZ), :]
         return c
 
     def whole_step(i, c):
@@ -652,21 +652,11 @@
             for t in TILES:
                 acc[t] = acc[t] + w * Z[k, t, pl.ds(r, NZ), :]
         for t in TILES:
-            X0[t, pl.ds(r, NZ), :] = acc[t]
+            out_ref[pl.ds(rowsof(i), NZ), LANES * t:LANES * t + LANES] = acc[t]
         return c
 
-    outs = []
-    for part in range(4):
-        if part < NQ:
-            lax.fori_loop(16 * part, min(16 * part + 16, AHEAD), last_step, 0, unroll=4)
-        if 16 * part + 16 > AHEAD:
-            lax.fori_loop(max(16 * part, AHEAD), 16 * part + 16, whole_step, 0, unroll=2)
-        for t in TILES:
-            cp = pltpu.make_async_copy(X0.at[t, pl.ds(NZ + 16 * NZ * part, 16 * NZ), :],
-                                       out_h.at[pl.ds(16 * NZ * part, 16 * NZ), pl.ds(LANES * t, LANES)],
-                                       osem.at[2 * part + t])
-            cp.start()
-            outs.append(cp)
+    lax.fori_loop(0, AHEAD, last_step, 0, unroll=4)
+    lax.fori_loop(AHEAD, NX, whole_step, 0, unroll=2)
 
     @pl.when(has_hi)
     def _():
@@ -705,8 +695,19 @@
         for cp in sum_copies(e):
             cp.wait_send()
 
-    for cp in outs:
-        cp.wait()
+
+def hand_over(src, dst, sem):
+    cp = pltpu.make_async_copy(src, dst, sem.at[0])
+    cp.start()
+    cp.wait()
+
+
+def publish(x_rows):
+    rows = pl.pallas_call(
+        hand_over, out_shape=jax.ShapeDtypeStruct(x_rows.shape, jnp.float32),
+        in_specs=[pl.BlockSpec(memory_space=pltpu.VMEM)], out_specs=pl.BlockSpec(memory_space=pl.ANY),
+        scratch_shapes=[pltpu.SemaphoreType.DMA((1,))])(x_rows)
+    return jnp.transpose(rows.reshape(NX, NZ, ROW), (0, 2, 1))
 
 
 def fused_solve(shift, rhs_field, x_init, cond_x, cond_y, cond_z):
@@ -717,9 +718,9 @@
     any_spec = pl.BlockSpec(memory_space=pl.ANY)
     x_rows, small = pl.pallas_call(
         kernel,
-        out_shape=(jax.ShapeDtypeStruct((BODY, 256), f32), jax.ShapeDtypeStruct(VREG, f32)),
+        out_shape=(pltpu.VMEM((BODY, 256), f32), jax.ShapeDtypeStruct(VREG, f32)),
         in_specs=[any_spec] * 6,
-        out_specs=(any_spec, pl.BlockSpec(memory_space=pltpu.VMEM)),
+        out_specs=(pl.BlockSpec(memory_space=pltpu.VMEM), pl.BlockSpec(memory_space=pltpu.VMEM)),
         scratch_shapes=[
             pltpu.VMEM((ITERS + 1, 2, FULL, LANES), f32),
             pltpu.VMEM((2, FULL, LANES), f32),
@@ -746,7 +747,6 @@
             pltpu.SemaphoreType.DMA((12,)),
             pltpu.SemaphoreType.DMA((8,)),
             pltpu.SemaphoreType.DMA((8,)),
-            pltpu.SemaphoreType.DMA((8,)),
             pltpu.SemaphoreType.DMA((ITERS, 5)),
             pltpu.SemaphoreType.DMA((ITERS, 5)),
             pltpu.SemaphoreType.DMA((ITERS + 1, TOP)),
@@ -755,8 +755,7 @@
         compiler_params=pltpu.CompilerParams(collective_id=0, has_side_effects=True,
                                              vmem_limit_bytes=65011712),
     )(*(flat(v) for v in (shift, rhs_field, x_init, cond_x, cond_y, cond_z)))
-    x_out = jnp.transpose(x_rows.reshape(NX, NZ, 256), (0, 2, 1))
-    return x_out, small[0, :ITERS + 1], small[1, 0]
+    return x_rows, small[0, :ITERS + 1], small[1, 0]
 
 
 def classic_solve(shift, rhs_field, x_init, cond_x, cond_y, cond_z):
@@ -823,8 +822,8 @@
     field_spec = P("px", "py", None)
 
     def local_solve(*fields):
-        x_out, history, err = fused_solve(*fields)
-        return lax.cond(err < ERR_LIMIT, lambda: (x_out, history), lambda: classic_solve(*fields))
+        x_rows, history, err = fused_solve(*fields)
+        return lax.cond(err < ERR_LIMIT, lambda: (publish(x_rows), history), lambda: classic_solve(*fields))
 
     return jax.shard_map(local_solve, mesh=mesh, in_specs=(field_spec,) * 6,
                          out_specs=(field_spec, P()), check_vma=False)

time: 79.9 us -> 78.4 us (0.981)
  local copies, waits for them, and re-layouts: 3.18 us -> 1.03 us
    unnamed x5 -> x0, local copies, waits for them, and re-layouts: 2.66 us -> none
    pallas_call x1 -> x2, Pallas kernels: 75 us -> 75.7 us  [the longest x1 74.6 us: fused_solve(): pl.pallas_call(kernel, out_shape=(pltpu.VMEM((BODY, 256), f32), jax.Shape...]
where the time goes in v6:
time: 78.4 us; the launch traced here: 78.3 us
  Pallas kernels  75.7 us (97%)
  between operations  1.29 us (2%)
  local copies, waits for them, and re-layouts  1.03 us (1%)
    pallas_call x1, Pallas kernels, fused_solve(): pl.pallas_call(kernel, out_shape=(pltpu.VMEM((BODY, 256), f32), jax.Shape...  74.6 us

profile of v6, /device:TPU:0, one launch (start us, length us, event | category | flops | bytes accessed | tf_op | source)
XLA Modules:
  0.0 78.3 jit_solution(9177936173008124528)
XLA Ops:
  0.6 74.6 %shard_map.81 = (f32[1536,256]{1,0:T(8,128)S(1)}, f32[8,128]{1,0:T(8,128)S(1)}) custom-call(f32[1536,256]{1,0:T(8,128)} %bitcast.33, f32[1536,256]{1,0:T(8,128)} %bitcast.34, f32[1536,256]{1,0:T(8,128)} %bitcast.26, f32[1536,256]{1,0:T(8,128)} %bitcast.30, f32[1536,256]{1,0:T(8,128)} %bitcast.31, f32[1536,256]{1,0:T(8,128)} %bitcast.32), custom_call_target="tpu_custom_call" | custom-call | tf_op jit(solution)/shard_map/pallas_call | solution.py:719
  75.2 0.5 slice.122
  76.4 1.9 %conditional.1 = (f32[64,256,24]{1,2,0:T(8,128)}, f32[21]{0:T(128)}) conditional(s32[]{:T(128)} %bitcast.16, (f32[64,256,24]{1,2,0:T(8,128)}, f32[64,256,24]{1,2,0:T(8,128)}, f32[64,256,24]{1,2,0:T(8,128)}, f32[64,256,24]{1,2,0:T(8,128)}, f32[64,256,24]{1,2,0:T(8,128)}, /*index=5*/f32[64,256,24]{1,2,0:T(8,128)}) %tuple.28, ...), branch_computations={%region_0.9_spmd, %region_9.10_spmd} | conditional | flops 28705548 | bytes 243432496 | solution.py:826
  76.6 1.2 %branch_1_fun.1 = f32[1536,256]{1,0:T(8,128)} custom-call(f32[1536,256]{1,0:T(8,128)S(1)} %get-tuple-element.239.src), custom_call_target="tpu_custom_call" | custom-call | tf_op jit(solution)/shard_map/cond/branch_1_fun/pallas_call | solution.py:706
  77.8 0.5 slice_bitcast_fusion

commit v7 on v6

--- a/solution.py
+++ b/solution.py
@@ -80,7 +80,7 @@
             to = Z.at[0, t, pl.ds(base, BODY), :] if dst is None else dst.at[t, pl.ds(base, BODY), :]
             cp = pltpu.make_async_copy(src.at[:, pl.ds(LANES * t, LANES)], to, lsem.at[2 * n + t])
             loads.append(cp)
-    for cp in loads[:4]:
+    for cp in loads:
         cp.start()
 
     zero_plane = jnp.zeros((NZ, LANES), jnp.float32)
@@ -186,8 +186,6 @@
 
     for cp in loads[:4]:
         cp.wait()
-    for cp in loads[4:]:
-        cp.start()
     pack(KY, 0, edge, KYP)
     ky_copy = remote(KYP, KYH, is_s.at[6], is_r.at[6], to_y)
 
@@ -611,7 +609,7 @@
         YB[k] = lane_sum(jnp.where(lane == k, y, NIL))
         YB[ITERS + k] = lane_sum(jnp.where(lane == k, d, NIL))
 
-    AHEAD = 32
+    AHEAD = 24
 
     def combine(i, c):
         r = rowsof(i + 1)

time: 78.4 us -> 77.3 us (0.986)
  Pallas kernels: 75.7 us -> 74.6 us
    pallas_call x1, Pallas kernels: 74.6 us -> 73.4 us  [fused_solve(): pl.pallas_call(kernel, out_shape=(pltpu.VMEM((BODY, 256), f32), jax.Shape...]
where the time goes in v7:
time: 77.3 us; the launch traced here: 77.2 us
  Pallas kernels  74.6 us (97%)
  between operations  1.29 us (2%)
  local copies, waits for them, and re-layouts  1.03 us (1%)
    pallas_call x1, Pallas kernels, fused_solve(): pl.pallas_call(kernel, out_shape=(pltpu.VMEM((BODY, 256), f32), jax.Shape...  73.4 us

profile of v7, /device:TPU:0, one launch (start us, length us, event | category | flops | bytes accessed | tf_op | source)
XLA Modules:
  0.0 77.2 jit_solution(2494438391901636678)
XLA Ops:
  0.6 73.4 %shard_map.81 = (f32[1536,256]{1,0:T(8,128)S(1)}, f32[8,128]{1,0:T(8,128)S(1)}) custom-call(f32[1536,256]{1,0:T(8,128)} %bitcast.33, f32[1536,256]{1,0:T(8,128)} %bitcast.34, f32[1536,256]{1,0:T(8,128)} %bitcast.26, f32[1536,256]{1,0:T(8,128)} %bitcast.30, f32[1536,256]{1,0:T(8,128)} %bitcast.31, f32[1536,256]{1,0:T(8,128)} %bitcast.32), custom_call_target="tpu_custom_call" | custom-call | tf_op jit(solution)/shard_map/pallas_call | solution.py:717
  74.1 0.5 slice.122
  75.3 1.9 %conditional.1 = (f32[64,256,24]{1,2,0:T(8,128)}, f32[21]{0:T(128)}) conditional(s32[]{:T(128)} %bitcast.16, (f32[64,256,24]{1,2,0:T(8,128)}, f32[64,256,24]{1,2,0:T(8,128)}, f32[64,256,24]{1,2,0:T(8,128)}, f32[64,256,24]{1,2,0:T(8,128)}, f32[64,256,24]{1,2,0:T(8,128)}, /*index=5*/f32[64,256,24]{1,2,0:T(8,128)}) %tuple.28, ...), branch_computations={%region_0.9_spmd, %region_9.10_spmd} | conditional | flops 28705548 | bytes 243432496 | solution.py:824
  75.5 1.2 %branch_1_fun.1 = f32[1536,256]{1,0:T(8,128)} custom-call(f32[1536,256]{1,0:T(8,128)S(1)} %get-tuple-element.239.src), custom_call_target="tpu_custom_call" | custom-call | tf_op jit(solution)/shard_map/cond/branch_1_fun/pallas_call | solution.py:704
  76.7 0.5 slice_bitcast_fusion
